TPU v7x, 32 devices: a whole 2x2x4 slice. The times are simulated.
32 devices in a mesh: gx: 2 (over core), gy: 4 (over y, x), gz: 4 (over z).
Axes of the slice: x: 2, y: 2, z: 4, core: 2. Of those that a mesh axis runs over, the one named last changes fastest.
Arguments:
- sources: float32 [1, 32, 64, 512], P(None, 'gx', 'gy', 'gz'), may hold values from -6 to 6
- stiffness: float32 [32, 64, 512], P('gx', 'gy', 'gz'), may hold values from 0.5 to 2
- coarse_inverse: float32 [256, 256], P(('gx', 'gy', 'gz')), may hold values from -6 to 6
Outputs:
- pressure: float32 [1, 32, 64, 512], P(None, 'gx', 'gy', 'gz')
All inputs are finite; a program needn't handle non-finite values.
Results may differ from a plain program's by a relative error of at most 0.0001.
Values sent between devices are 32-bit elements; how exact they have to be, the bound alone decides.
A program may use at most 64 MiB of HBM per device.

v0:
```python
import jax
import jax.numpy as jnp
from jax import lax
from jax.sharding import PartitionSpec as P

damping = 0.8


def extended(cells, sides, width):
    for axis, dim in sides:
        count = lax.axis_size(axis)
        ends = count - 1
        head = lax.slice_in_dim(cells, 0, width, axis=dim)
        tail = lax.slice_in_dim(cells, cells.shape[dim] - width, cells.shape[dim], axis=dim)
        cells = jnp.concatenate(
            [
                lax.ppermute(tail, axis, [(i, (i + 1) % count) for i in range(ends)]),
                cells,
                lax.ppermute(head, axis, [((i + 1) % count, i) for i in range(ends)]),
            ],
            axis=dim,
        )
    return cells


def loop_sum(padded):
    total = padded[:, 2:, 1:-1, 1:-1] + padded[:, :-2, 1:-1, 1:-1]
    total = total + padded[:, 1:-1, 2:, 1:-1] + padded[:, 1:-1, :-2, 1:-1]
    total = total + padded[:, 1:-1, 1:-1, 2:] + padded[:, 1:-1, 1:-1, :-2]
    return total


def inner_part(values):
    return values[:, 1:-1, 1:-1, 1:-1]


def pre_smooth(source, weights):
    count = source.shape[0]
    stacked = jnp.concatenate([source, weights], axis=0)
    wide = extended(stacked, (("gx", 1), ("gy", 2), ("gz", 3)), 2)
    wide_source = wide[:count]
    wide_weights = wide[count:]
    safe_weights = jnp.where(wide_weights > 0.0, wide_weights, 1.0)
    first = damping * wide_source / (6.0 * safe_weights * safe_weights)
    first_scaled = wide_weights * first
    mid_weights = inner_part(wide_weights)
    mid_safe = inner_part(safe_weights)
    applied = mid_weights * (6.0 * inner_part(first_scaled) - loop_sum(first_scaled))
    second = inner_part(first) + damping * (inner_part(wide_source) - applied) / (
        6.0 * mid_safe * mid_safe
    )
    second_scaled = mid_weights * second
    answer = inner_part(second)
    resid = source - weights * (6.0 * inner_part(second_scaled) - loop_sum(second_scaled))
    return (answer, resid)


def post_smooth(answer, source, weights):
    scaled = weights * answer
    wide = extended(scaled, (("gx", 1), ("gy", 2), ("gz", 3)), 1)
    applied = weights * (6.0 * scaled - loop_sum(wide))
    return answer + damping * (source - applied) / (6.0 * weights * weights)


def coarsen(values):
    leading = values.shape[0]
    size_x, size_y, size_z = (values.shape[1], values.shape[2], values.shape[3])
    blocks = values.reshape((leading, size_x // 2, 2, size_y // 2, 2, size_z // 2, 2))
    return jnp.mean(blocks, axis=(2, 4, 6))


def refine(values):
    return jnp.repeat(jnp.repeat(jnp.repeat(values, 2, axis=1), 2, axis=2), 2, axis=3)


def per_device(sources, stiffness, coarse_inverse):
    weight_list = [stiffness[None]]
    for level in range(3):
        weight_list.append(0.5 * coarsen(weight_list[-1]))
    source_list = []
    answer_list = []
    current = sources
    for level in range(4):
        source_list.append(current)
        answer, resid = pre_smooth(current, weight_list[level])
        answer_list.append(answer)
        current = coarsen(resid)
    count = current.shape[0]
    flat_source = current.reshape((count, -1))
    solved = lax.dot_general(
        lax.all_gather(flat_source, ("gx", "gy", "gz"), axis=1, tiled=True),
        coarse_inverse,
        (((1,), (1,)), ((), ())),
        precision=lax.Precision.HIGHEST,
        preferred_element_type=jnp.float32,
    )
    correction = solved.reshape(current.shape)
    for level in range(3, -1, -1):
        correction = post_smooth(
            answer_list[level] + refine(correction), source_list[level], weight_list[level]
        )
    return correction


def solution(mesh):
    in_specs = (P(None, "gx", "gy", "gz"), P("gx", "gy", "gz"), P(("gx", "gy", "gz"), None))
    out_specs = P(None, "gx", "gy", "gz")
    return jax.shard_map(
        per_device, mesh=mesh, in_specs=in_specs, out_specs=out_specs, check_vma=False
    )
```

profile of v0, /device:TPU:0, one launch (start us, length us, event | category | flops | bytes accessed | tf_op | source)
XLA Modules:
  0.0 273.9 jit_solution(9467583034794513694)
XLA Ops:
  0.8 2.4 collective-permute-start
  3.2 1.3 collective-permute-start.1
  4.5 1.8 collective-permute-done.1
  7.3 4.2 %collective-permute-start.2 = (f32[2,20,2,128]{3,2,1,0:T(2,128)S(1)}, f32[2,20,2,128]{3,2,1,0:T(2,128)S(1)}, u32[]{:S(2)}, u32[]{:S(2)}) collective-permute-start(f32[2,20,2,128]{3,2,1,0:T(2,128)S(1)} %get-tuple-element.27), channel_id=1, source_target_pairs={{0,4},{4,8},{8,12},{1,5},{5,9},{9,13},{2,6},{6,10},{10,14},{3,7},{... | collective-permute-start | bytes 122888 | tf_op jit(solution)/shard_map/ppermute | solution.py:17
  11.5 10.5 %reshape_broadcast_in_dim.3 = f32[8,2,8,2,64,2]{5,4,3,2,1,0:T(8,128)} reshape(f32[16,16,128]{2,1,0:T(8,128)} %param.4) | data formatting | bytes 262144 | tf_op jit(solution)/shard_map/reshape;broadcast_in_dim | solution.py:68
  22.1 4.0 %reduce_sum.71 = f32[8,8,64]{2,1,0:T(8,128)S(1)} reduce(f32[8,2,8,2,64,2]{5,4,3,2,1,0:T(8,128)} %reshape_broadcast_in_dim.3, f32[]{:T(128)} %constant.14.clone.1), dimensions={1,3,5}, to_apply=%region_1.0 | reduce | flops 28672 | bytes 147460 | tf_op jit(solution)/shard_map/reduce_sum | solution.py:69
  26.1 1.4 collective-permute-start.3
  27.9 4.3 %collective-permute-done.3 = f32[2,20,2,128]{3,2,1,0:T(2,128)S(1)} collective-permute-done((f32[2,20,2,128]{3,2,1,0:T(2,128)S(1)}, f32[2,20,2,128]{3,2,1,0:T(2,128)S(1)}, u32[]{:S(2)}, u32[]{:S(2)}) %collective-permute-start.3) | collective-permute-done | bytes 40992 | tf_op jit(solution)/shard_map/ppermute | solution.py:19
  32.7 3.5 %collective-permute-start.4 = (f32[2,20,20,2]{3,0,2,1:T(2,128)S(1)}, f32[2,20,20,2]{3,0,2,1:T(2,128)S(1)}, u32[]{:S(2)}, u32[]{:S(2)}) collective-permute-start(f32[2,20,20,2]{3,0,2,1:T(2,128)S(1)} %get-tuple-element.24), channel_id=1, source_target_pairs={{0,1},{1,2},{2,3},{4,5},{5,6},{6,7},{8,9},{9,10},{10,11},{12,13},{... | collective-permute-start | bytes 19208 | tf_op jit(solution)/shard_map/ppermute | solution.py:17
  36.2 1.3 collective-permute-start.5
  37.5 6.3 %collective-permute-done.4 = f32[2,20,20,2]{3,0,2,1:T(2,128)S(1)} collective-permute-done((f32[2,20,20,2]{3,0,2,1:T(2,128)S(1)}, f32[2,20,20,2]{3,0,2,1:T(2,128)S(1)}, u32[]{:S(2)}, u32[]{:S(2)}) %collective-permute-start.4) | collective-permute-done | bytes 6432 | tf_op jit(solution)/shard_map/ppermute | solution.py:17
  43.7 4.1 %collective-permute-done.5 = f32[2,20,20,2]{3,0,2,1:T(2,128)S(1)} collective-permute-done((f32[2,20,20,2]{3,0,2,1:T(2,128)S(1)}, f32[2,20,20,2]{3,0,2,1:T(2,128)S(1)}, u32[]{:S(2)}, u32[]{:S(2)}) %collective-permute-start.5) | collective-permute-done | bytes 6432 | tf_op jit(solution)/shard_map/ppermute | solution.py:19
  47.9 1.3 pad_maximum_fusion
  49.9 1.4 fusion.95
  52.8 9.8 %reshape.211 = f32[8,2,8,2,64,2]{5,4,3,2,1,0:T(8,128)} reshape(f32[1,16,16,128]{3,2,1,0:T(8,128)S(1)} %fusion.20) | data formatting | bytes 262144 | tf_op jit(solution)/shard_map/reshape | solution.py:68
  62.6 4.0 %reduce_sum.70 = f32[8,8,64]{2,1,0:T(8,128)S(1)} reduce(f32[8,2,8,2,64,2]{5,4,3,2,1,0:T(8,128)} %reshape.211, f32[]{:T(128)} %constant.14.clone.1), dimensions={1,3,5}, to_apply=%region_0.0 | reduce | flops 28672 | bytes 147460 | tf_op jit(solution)/shard_map/reduce_sum | solution.py:69
  67.9 1.3 collective-permute-start.7
  69.2 1.8 collective-permute-done.7
  71.0 4.3 %collective-permute-start.8 = (f32[2,12,2,64]{3,2,1,0:T(2,128)S(1)}, f32[2,12,2,64]{3,2,1,0:T(2,128)S(1)}, u32[]{:S(2)}, u32[]{:S(2)}) collective-permute-start(f32[2,12,2,64]{3,2,1,0:T(2,128)S(1)} %get-tuple-element.47), channel_id=1, source_target_pairs={{0,4},{4,8},{8,12},{1,5},{5,9},{9,13},{2,6},{6,10},{10,14},{3,7},{... | collective-permute-start | bytes 36872 | tf_op jit(solution)/shard_map/ppermute | solution.py:17
  76.6 1.3 collective-permute-start.9
  78.0 4.3 %collective-permute-done.9 = f32[2,12,2,64]{3,2,1,0:T(2,128)S(1)} collective-permute-done((f32[2,12,2,64]{3,2,1,0:T(2,128)S(1)}, f32[2,12,2,64]{3,2,1,0:T(2,128)S(1)}, u32[]{:S(2)}, u32[]{:S(2)}) %collective-permute-start.9) | collective-permute-done | bytes 12320 | tf_op jit(solution)/shard_map/ppermute | solution.py:19
  82.5 3.5 %collective-permute-start.10 = (f32[2,12,12,2]{3,0,2,1:T(2,128)S(1)}, f32[2,12,12,2]{3,0,2,1:T(2,128)S(1)}, u32[]{:S(2)}, u32[]{:S(2)}) collective-permute-start(f32[2,12,12,2]{3,0,2,1:T(2,128)S(1)} %get-tuple-element.42), channel_id=1, source_target_pairs={{0,1},{1,2},{2,3},{4,5},{5,6},{6,7},{8,9},{9,10},{10,11},{12,13},{... | collective-permute-start | bytes 6920 | tf_op jit(solution)/shard_map/ppermute | solution.py:17
  86.0 1.5 collective-permute-start.11
  88.6 4.4 %collective-permute-done.11 = f32[2,12,12,2]{3,0,2,1:T(2,128)S(1)} collective-permute-done((f32[2,12,12,2]{3,0,2,1:T(2,128)S(1)}, f32[2,12,12,2]{3,0,2,1:T(2,128)S(1)}, u32[]{:S(2)}, u32[]{:S(2)}) %collective-permute-start.11) | collective-permute-done | bytes 2336 | tf_op jit(solution)/shard_map/ppermute | solution.py:19
  96.8 1.3 collective-permute-start.13
  98.1 1.8 collective-permute-done.13
  99.9 3.4 %collective-permute-start.14 = (f32[2,8,2,32]{3,2,1,0:T(2,128)S(1)}, f32[2,8,2,32]{3,2,1,0:T(2,128)S(1)}, u32[]{:S(2)}, u32[]{:S(2)}) collective-permute-start(f32[2,8,2,32]{3,2,1,0:T(2,128)S(1)} %get-tuple-element.65), channel_id=1, source_target_pairs={{0,4},{4,8},{8,12},{1,5},{5,9},{9,13},{2,6},{6,10},{10,14},{3,7},{... | collective-permute-start | bytes 12296 | tf_op jit(solution)/shard_map/ppermute | solution.py:17
  103.3 1.3 collective-permute-start.15
  104.7 4.2 %collective-permute-done.15 = f32[2,8,2,32]{3,2,1,0:T(2,128)S(1)} collective-permute-done((f32[2,8,2,32]{3,2,1,0:T(2,128)S(1)}, f32[2,8,2,32]{3,2,1,0:T(2,128)S(1)}, u32[]{:S(2)}, u32[]{:S(2)}) %collective-permute-start.15) | collective-permute-done | bytes 4128 | tf_op jit(solution)/shard_map/ppermute | solution.py:19
  109.1 3.5 %collective-permute-start.16 = (f32[2,8,8,2]{3,2,1,0:T(8,128)S(1)}, f32[2,8,8,2]{3,2,1,0:T(8,128)S(1)}, u32[]{:S(2)}, u32[]{:S(2)}) collective-permute-start(f32[2,8,8,2]{3,2,1,0:T(8,128)S(1)} %get-tuple-element.50), channel_id=1, source_target_pairs={{0,1},{1,2},{2,3},{4,5},{5,6},{6,7},{8,9},{9,10},{10,11},{12,13},{... | collective-permute-start | bytes 3080 | tf_op jit(solution)/shard_map/ppermute | solution.py:17
  112.5 1.3 collective-permute-start.17
  114.4 4.3 %collective-permute-done.17 = f32[2,8,8,2]{3,2,1,0:T(8,128)S(1)} collective-permute-done((f32[2,8,8,2]{3,2,1,0:T(8,128)S(1)}, f32[2,8,8,2]{3,2,1,0:T(8,128)S(1)}, u32[]{:S(2)}, u32[]{:S(2)}) %collective-permute-start.17) | collective-permute-done | bytes 1056 | tf_op jit(solution)/shard_map/ppermute | solution.py:19
  120.6 1.3 collective-permute-start.19
  121.9 1.8 collective-permute-done.19
  123.7 2.8 %collective-permute-start.20 = (f32[2,6,2,16]{3,2,1,0:T(2,128)S(1)}, f32[2,6,2,16]{3,2,1,0:T(2,128)S(1)}, u32[]{:S(2)}, u32[]{:S(2)}) collective-permute-start(f32[2,6,2,16]{3,2,1,0:T(2,128)S(1)} %pad_maximum_fusion.46), channel_id=1, source_target_pairs={{0,4},{4,8},{8,12},{1,5},{5,9},{9,13},{2,6},{6,10},{10,14},{3,7},{... | collective-permute-start | bytes 4616 | tf_op jit(solution)/shard_map/ppermute | solution.py:17
  126.5 1.3 collective-permute-start.21
  127.9 4.2 %collective-permute-done.21 = f32[2,6,2,16]{3,2,1,0:T(2,128)S(1)} collective-permute-done((f32[2,6,2,16]{3,2,1,0:T(2,128)S(1)}, f32[2,6,2,16]{3,2,1,0:T(2,128)S(1)}, u32[]{:S(2)}, u32[]{:S(2)}) %collective-permute-start.21) | collective-permute-done | bytes 1568 | tf_op jit(solution)/shard_map/ppermute | solution.py:19
  132.2 1.9 collective-permute-start.22
  134.2 1.3 collective-permute-start.23
  135.9 4.3 %collective-permute-done.23 = f32[2,6,6,2]{3,2,1,0:T(8,128)S(1)} collective-permute-done((f32[2,6,6,2]{3,2,1,0:T(8,128)S(1)}, f32[2,6,6,2]{3,2,1,0:T(8,128)S(1)}, u32[]{:S(2)}, u32[]{:S(2)}) %collective-permute-start.23) | collective-permute-done | bytes 608 | tf_op jit(solution)/shard_map/ppermute | solution.py:19
  140.8 37.6 %all-reduce = f32[256]{0:T(256)S(1)} all-reduce(f32[256]{0:T(256)S(1)} %multiply_dynamic-update-slice_fusion), channel_id=2, replica_groups=mesh['gx'=2,'gy'=4,'gz'=4] {'gx','gy','gz'}, use_global_device_ids=true, to_apply=%add | all-reduce | flops 256 | bytes 2048
  178.8 1.3 collective-permute-start.24
  180.1 3.0 %collective-permute-start.25 = (f32[1,1,2,16]{3,2,1,0:T(2,128)S(1)}, f32[1,1,2,16]{3,2,1,0:T(2,128)S(1)}, u32[]{:S(2)}, u32[]{:S(2)}) collective-permute-start(f32[1,1,2,16]{3,2,1,0:T(2,128)S(1)} %get-tuple-element.85), channel_id=1, source_target_pairs={{0,16},{1,17},{2,18},{3,19},{4,20},{5,21},{6,22},{7,23},{8,24},{9,... | collective-permute-start | bytes 392 | tf_op jit(solution)/shard_map/ppermute | solution.py:17
  185.3 4.8 %collective-permute-start.27 = (f32[1,4,1,16]{3,2,1,0:T(1,128)S(1)}, f32[1,4,1,16]{3,2,1,0:T(1,128)S(1)}, u32[]{:S(2)}, u32[]{:S(2)}) collective-permute-start(f32[1,4,1,16]{3,2,1,0:T(1,128)S(1)} %get-tuple-element.83), channel_id=1, source_target_pairs={{0,4},{4,8},{8,12},{1,5},{5,9},{9,13},{2,6},{6,10},{10,14},{3,7},{... | collective-permute-start | bytes 776 | tf_op jit(solution)/shard_map/ppermute | solution.py:17
  192.8 4.6 %collective-permute-start.29 = (f32[1,4,4,1]{3,2,1,0:T(4,128)S(1)}, f32[1,4,4,1]{3,2,1,0:T(4,128)S(1)}, u32[]{:S(2)}, u32[]{:S(2)}) collective-permute-start(f32[1,4,4,1]{3,2,1,0:T(4,128)S(1)} %get-tuple-element.80), channel_id=1, source_target_pairs={{0,1},{1,2},{2,3},{4,5},{5,6},{6,7},{8,9},{9,10},{10,11},{12,13},{... | collective-permute-start | bytes 200 | tf_op jit(solution)/shard_map/ppermute | solution.py:17
  197.4 1.3 collective-permute-done.29
  200.4 3.0 %collective-permute-start.31 = (f32[1,1,4,32]{3,2,1,0:T(4,128)S(1)}, f32[1,1,4,32]{3,2,1,0:T(4,128)S(1)}, u32[]{:S(2)}, u32[]{:S(2)}) collective-permute-start(f32[1,1,4,32]{3,2,1,0:T(4,128)S(1)} %get-tuple-element.77), channel_id=1, source_target_pairs={{0,16},{1,17},{2,18},{3,19},{4,20},{5,21},{6,22},{7,23},{8,24},{9,... | collective-permute-start | bytes 1544 | tf_op jit(solution)/shard_map/ppermute | solution.py:17
  204.3 4.8 %collective-permute-start.33 = (f32[1,6,1,32]{3,2,1,0:T(1,128)S(1)}, f32[1,6,1,32]{3,2,1,0:T(1,128)S(1)}, u32[]{:S(2)}, u32[]{:S(2)}) collective-permute-start(f32[1,6,1,32]{3,2,1,0:T(1,128)S(1)} %get-tuple-element.75), channel_id=1, source_target_pairs={{0,4},{4,8},{8,12},{1,5},{5,9},{9,13},{2,6},{6,10},{10,14},{3,7},{... | collective-permute-start | bytes 2312 | tf_op jit(solution)/shard_map/ppermute | solution.py:17
  209.1 1.3 collective-permute-start.32
  210.4 5.3 %collective-permute-done.32 = f32[1,6,1,32]{3,2,1,0:T(1,128)S(1)} collective-permute-done((f32[1,6,1,32]{3,2,1,0:T(1,128)S(1)}, f32[1,6,1,32]{3,2,1,0:T(1,128)S(1)}, u32[]{:S(2)}, u32[]{:S(2)}) %collective-permute-start.32) | collective-permute-done | bytes 800 | tf_op jit(solution)/shard_map/ppermute | solution.py:19
  215.9 1.3 collective-permute-start.34
  217.2 4.8 %collective-permute-start.35 = (f32[1,6,6,1]{3,0,2,1:T(1,128)S(1)}, f32[1,6,6,1]{3,0,2,1:T(1,128)S(1)}, u32[]{:S(2)}, u32[]{:S(2)}) collective-permute-start(f32[1,6,6,1]{3,0,2,1:T(1,128)S(1)} %get-tuple-element.72), channel_id=1, source_target_pairs={{0,1},{1,2},{2,3},{4,5},{5,6},{6,7},{8,9},{9,10},{10,11},{12,13},{... | collective-permute-start | bytes 440 | tf_op jit(solution)/shard_map/ppermute | solution.py:17
  222.0 1.4 collective-permute-done.35
  225.4 3.0 %collective-permute-start.37 = (f32[1,1,8,64]{3,2,1,0:T(8,128)S(1)}, f32[1,1,8,64]{3,2,1,0:T(8,128)S(1)}, u32[]{:S(2)}, u32[]{:S(2)}) collective-permute-start(f32[1,1,8,64]{3,2,1,0:T(8,128)S(1)} %get-tuple-element.63), channel_id=1, source_target_pairs={{0,16},{1,17},{2,18},{3,19},{4,20},{5,21},{6,22},{7,23},{8,24},{9,... | collective-permute-start | bytes 6152 | tf_op jit(solution)/shard_map/ppermute | solution.py:17
  229.2 4.8 %collective-permute-start.39 = (f32[1,10,1,64]{3,2,1,0:T(1,128)S(1)}, f32[1,10,1,64]{3,2,1,0:T(1,128)S(1)}, u32[]{:S(2)}, u32[]{:S(2)}) collective-permute-start(f32[1,10,1,64]{3,2,1,0:T(1,128)S(1)} %get-tuple-element.61), channel_id=1, source_target_pairs={{0,4},{4,8},{8,12},{1,5},{5,9},{9,13},{2,6},{6,10},{10,14},{3,7},{... | collective-permute-start | bytes 7688 | tf_op jit(solution)/shard_map/ppermute | solution.py:17
  235.4 4.2 %collective-permute-done.38 = f32[1,10,1,64]{3,2,1,0:T(1,128)S(1)} collective-permute-done((f32[1,10,1,64]{3,2,1,0:T(1,128)S(1)}, f32[1,10,1,64]{3,2,1,0:T(1,128)S(1)}, u32[]{:S(2)}, u32[]{:S(2)}) %collective-permute-start.38) | collective-permute-done | bytes 2592 | tf_op jit(solution)/shard_map/ppermute | solution.py:19
  241.1 4.8 %collective-permute-start.41 = (f32[1,10,10,1]{3,0,2,1:T(1,128)S(1)}, f32[1,10,10,1]{3,0,2,1:T(1,128)S(1)}, u32[]{:S(2)}, u32[]{:S(2)}) collective-permute-start(f32[1,10,10,1]{3,0,2,1:T(1,128)S(1)} %get-tuple-element.57), channel_id=1, source_target_pairs={{0,1},{1,2},{2,3},{4,5},{5,6},{6,7},{8,9},{9,10},{10,11},{12,13},{... | collective-permute-start | bytes 1208 | tf_op jit(solution)/shard_map/ppermute | solution.py:17
  246.1 1.6 collective-permute-done.41
  250.4 3.0 %collective-permute-start.43 = (f32[1,1,16,128]{3,2,1,0:T(8,128)S(1)}, f32[1,1,16,128]{3,2,1,0:T(8,128)S(1)}, u32[]{:S(2)}, u32[]{:S(2)}) collective-permute-start(f32[1,1,16,128]{3,2,1,0:T(8,128)S(1)} %get-tuple-element.44), channel_id=1, source_target_pairs={{0,16},{1,17},{2,18},{3,19},{4,20},{5,21},{6,22},{7,23},{8,24},{9,... | collective-permute-start | bytes 24584 | tf_op jit(solution)/shard_map/ppermute | solution.py:17
  254.2 2.8 %collective-permute-start.45 = (f32[1,18,1,128]{3,2,1,0:T(1,128)S(1)}, f32[1,18,1,128]{3,2,1,0:T(1,128)S(1)}, u32[]{:S(2)}, u32[]{:S(2)}) collective-permute-start(f32[1,18,1,128]{3,2,1,0:T(1,128)S(1)} %get-tuple-element.34), channel_id=1, source_target_pairs={{0,4},{4,8},{8,12},{1,5},{5,9},{9,13},{2,6},{6,10},{10,14},{3,7},{... | collective-permute-start | bytes 27656 | tf_op jit(solution)/shard_map/ppermute | solution.py:17
  258.4 4.2 %collective-permute-done.44 = f32[1,18,1,128]{3,2,1,0:T(1,128)S(1)} collective-permute-done((f32[1,18,1,128]{3,2,1,0:T(1,128)S(1)}, f32[1,18,1,128]{3,2,1,0:T(1,128)S(1)}, u32[]{:S(2)}, u32[]{:S(2)}) %collective-permute-start.44) | collective-permute-done | bytes 9248 | tf_op jit(solution)/shard_map/ppermute | solution.py:19
  264.5 4.9 %collective-permute-start.47 = (f32[1,18,18,1]{3,0,2,1:T(1,128)S(1)}, f32[1,18,18,1]{3,0,2,1:T(1,128)S(1)}, u32[]{:S(2)}, u32[]{:S(2)}) collective-permute-start(f32[1,18,18,1]{3,0,2,1:T(1,128)S(1)} %get-tuple-element.33), channel_id=1, source_target_pairs={{0,1},{1,2},{2,3},{4,5},{5,6},{6,7},{8,9},{9,10},{10,11},{12,13},{... | collective-permute-start | bytes 3896 | tf_op jit(solution)/shard_map/ppermute | solution.py:17
  269.4 1.4 collective-permute-done.46
  270.7 1.5 collective-permute-done.47
  (154 shorter events, 38.2 us)
Async XLA Ops:
  0.0 178.5 %copy-start = (f32[8,256]{1,0:T(8,128)S(1)}, f32[8,256]{1,0:T(8,128)}, u32[]{:S(2)}) copy-start(f32[8,256]{1,0:T(8,128)} %param.5) | copy-start | bytes 24580
  0.8 3.7 %collective-permute-start = (f32[2,2,16,128]{3,2,1,0:T(8,128)S(1)}, f32[2,2,16,128]{3,2,1,0:T(8,128)S(1)}, u32[]{:S(2)}, u32[]{:S(2)}) collective-permute-start(f32[2,2,16,128]{3,2,1,0:T(8,128)S(1)} %get-tuple-element.28), channel_id=1, source_target_pairs={{0,16},{1,17},{2,18},{3,19},{4,20},{5,21},{6,22},{7,23},{8,24},{9,... | collective-permute-start | bytes 98312 | tf_op jit(solution)/shard_map/ppermute | solution.py:17
  3.2 3.1 %collective-permute-start.1 = (f32[2,2,16,128]{3,2,1,0:T(8,128)S(1)}, f32[2,2,16,128]{3,2,1,0:T(8,128)S(1)}, u32[]{:S(2)}, u32[]{:S(2)}) collective-permute-start(f32[2,2,16,128]{3,2,1,0:T(8,128)S(1)} %get-tuple-element.29), channel_id=1, source_target_pairs={{16,0},{17,1},{18,2},{19,3},{20,4},{21,5},{22,6},{23,7},{24,8},{25... | collective-permute-start | bytes 98312 | tf_op jit(solution)/shard_map/ppermute | solution.py:19
  7.3 20.2 %collective-permute-start.2 = (f32[2,20,2,128]{3,2,1,0:T(2,128)S(1)}, f32[2,20,2,128]{3,2,1,0:T(2,128)S(1)}, u32[]{:S(2)}, u32[]{:S(2)}) collective-permute-start(f32[2,20,2,128]{3,2,1,0:T(2,128)S(1)} %get-tuple-element.27), channel_id=1, source_target_pairs={{0,4},{4,8},{8,12},{1,5},{5,9},{9,13},{2,6},{6,10},{10,14},{3,7},{... | collective-permute-start | bytes 122888 | tf_op jit(solution)/shard_map/ppermute | solution.py:17
  26.1 26.4 %copy-start.1 = (f32[16,16,128]{2,1,0:T(8,128)S(1)}, f32[16,16,128]{2,1,0:T(8,128)}, u32[]{:S(2)}) copy-start(f32[16,16,128]{2,1,0:T(8,128)} %param.4) | copy-start | bytes 393220
  26.1 26.4 %copy-start.2 = (f32[1,16,16,128]{3,2,1,0:T(8,128)S(1)}, f32[1,16,16,128]{3,2,1,0:T(8,128)}, u32[]{:S(2)}) copy-start(f32[1,16,16,128]{3,2,1,0:T(8,128)} %param.3) | copy-start | bytes 393220
  26.1 6.0 %collective-permute-start.3 = (f32[2,20,2,128]{3,2,1,0:T(2,128)S(1)}, f32[2,20,2,128]{3,2,1,0:T(2,128)S(1)}, u32[]{:S(2)}, u32[]{:S(2)}) collective-permute-start(f32[2,20,2,128]{3,2,1,0:T(2,128)S(1)} %get-tuple-element.26), channel_id=1, source_target_pairs={{4,0},{8,4},{12,8},{5,1},{9,5},{13,9},{6,2},{10,6},{14,10},{7,3},{... | collective-permute-start | bytes 122888 | tf_op jit(solution)/shard_map/ppermute | solution.py:19
  32.7 11.1 %collective-permute-start.4 = (f32[2,20,20,2]{3,0,2,1:T(2,128)S(1)}, f32[2,20,20,2]{3,0,2,1:T(2,128)S(1)}, u32[]{:S(2)}, u32[]{:S(2)}) collective-permute-start(f32[2,20,20,2]{3,0,2,1:T(2,128)S(1)} %get-tuple-element.24), channel_id=1, source_target_pairs={{0,1},{1,2},{2,3},{4,5},{5,6},{6,7},{8,9},{9,10},{10,11},{12,13},{... | collective-permute-start | bytes 19208 | tf_op jit(solution)/shard_map/ppermute | solution.py:17
  36.2 11.7 %collective-permute-start.5 = (f32[2,20,20,2]{3,0,2,1:T(2,128)S(1)}, f32[2,20,20,2]{3,0,2,1:T(2,128)S(1)}, u32[]{:S(2)}, u32[]{:S(2)}) collective-permute-start(f32[2,20,20,2]{3,0,2,1:T(2,128)S(1)} %get-tuple-element.25), channel_id=1, source_target_pairs={{1,0},{2,1},{3,2},{5,4},{6,5},{7,6},{9,8},{10,9},{11,10},{13,12},{... | collective-permute-start | bytes 19208 | tf_op jit(solution)/shard_map/ppermute | solution.py:19
  66.6 2.6 collective-permute-start.6
  67.9 3.1 %collective-permute-start.7 = (f32[2,2,8,64]{3,2,1,0:T(8,128)S(1)}, f32[2,2,8,64]{3,2,1,0:T(8,128)S(1)}, u32[]{:S(2)}, u32[]{:S(2)}) collective-permute-start(f32[2,2,8,64]{3,2,1,0:T(8,128)S(1)} %get-tuple-element.53), channel_id=1, source_target_pairs={{16,0},{17,1},{18,2},{19,3},{20,4},{21,5},{22,6},{23,7},{24,8},{25... | collective-permute-start | bytes 24584 | tf_op jit(solution)/shard_map/ppermute | solution.py:19
  71.0 6.8 %collective-permute-start.8 = (f32[2,12,2,64]{3,2,1,0:T(2,128)S(1)}, f32[2,12,2,64]{3,2,1,0:T(2,128)S(1)}, u32[]{:S(2)}, u32[]{:S(2)}) collective-permute-start(f32[2,12,2,64]{3,2,1,0:T(2,128)S(1)} %get-tuple-element.47), channel_id=1, source_target_pairs={{0,4},{4,8},{8,12},{1,5},{5,9},{9,13},{2,6},{6,10},{10,14},{3,7},{... | collective-permute-start | bytes 36872 | tf_op jit(solution)/shard_map/ppermute | solution.py:17
  76.6 5.7 %collective-permute-start.9 = (f32[2,12,2,64]{3,2,1,0:T(2,128)S(1)}, f32[2,12,2,64]{3,2,1,0:T(2,128)S(1)}, u32[]{:S(2)}, u32[]{:S(2)}) collective-permute-start(f32[2,12,2,64]{3,2,1,0:T(2,128)S(1)} %get-tuple-element.46), channel_id=1, source_target_pairs={{4,0},{8,4},{12,8},{5,1},{9,5},{13,9},{6,2},{10,6},{14,10},{7,3},{... | collective-permute-start | bytes 36872 | tf_op jit(solution)/shard_map/ppermute | solution.py:19
  82.5 6.1 %collective-permute-start.10 = (f32[2,12,12,2]{3,0,2,1:T(2,128)S(1)}, f32[2,12,12,2]{3,0,2,1:T(2,128)S(1)}, u32[]{:S(2)}, u32[]{:S(2)}) collective-permute-start(f32[2,12,12,2]{3,0,2,1:T(2,128)S(1)} %get-tuple-element.42), channel_id=1, source_target_pairs={{0,1},{1,2},{2,3},{4,5},{5,6},{6,7},{8,9},{9,10},{10,11},{12,13},{... | collective-permute-start | bytes 6920 | tf_op jit(solution)/shard_map/ppermute | solution.py:17
  86.0 7.0 %collective-permute-start.11 = (f32[2,12,12,2]{3,0,2,1:T(2,128)S(1)}, f32[2,12,12,2]{3,0,2,1:T(2,128)S(1)}, u32[]{:S(2)}, u32[]{:S(2)}) collective-permute-start(f32[2,12,12,2]{3,0,2,1:T(2,128)S(1)} %get-tuple-element.43), channel_id=1, source_target_pairs={{1,0},{2,1},{3,2},{5,4},{6,5},{7,6},{9,8},{10,9},{11,10},{13,12},{... | collective-permute-start | bytes 6920 | tf_op jit(solution)/shard_map/ppermute | solution.py:19
  95.5 2.6 collective-permute-start.12
  96.8 3.1 %collective-permute-start.13 = (f32[2,2,4,32]{3,2,1,0:T(4,128)S(1)}, f32[2,2,4,32]{3,2,1,0:T(4,128)S(1)}, u32[]{:S(2)}, u32[]{:S(2)}) collective-permute-start(f32[2,2,4,32]{3,2,1,0:T(4,128)S(1)} %get-tuple-element.74), channel_id=1, source_target_pairs={{16,0},{17,1},{18,2},{19,3},{20,4},{21,5},{22,6},{23,7},{24,8},{25... | collective-permute-start | bytes 6152 | tf_op jit(solution)/shard_map/ppermute | solution.py:19
  99.9 4.8 %collective-permute-start.14 = (f32[2,8,2,32]{3,2,1,0:T(2,128)S(1)}, f32[2,8,2,32]{3,2,1,0:T(2,128)S(1)}, u32[]{:S(2)}, u32[]{:S(2)}) collective-permute-start(f32[2,8,2,32]{3,2,1,0:T(2,128)S(1)} %get-tuple-element.65), channel_id=1, source_target_pairs={{0,4},{4,8},{8,12},{1,5},{5,9},{9,13},{2,6},{6,10},{10,14},{3,7},{... | collective-permute-start | bytes 12296 | tf_op jit(solution)/shard_map/ppermute | solution.py:17
  103.3 5.6 %collective-permute-start.15 = (f32[2,8,2,32]{3,2,1,0:T(2,128)S(1)}, f32[2,8,2,32]{3,2,1,0:T(2,128)S(1)}, u32[]{:S(2)}, u32[]{:S(2)}) collective-permute-start(f32[2,8,2,32]{3,2,1,0:T(2,128)S(1)} %get-tuple-element.66), channel_id=1, source_target_pairs={{4,0},{8,4},{12,8},{5,1},{9,5},{13,9},{6,2},{10,6},{14,10},{7,3},{... | collective-permute-start | bytes 12296 | tf_op jit(solution)/shard_map/ppermute | solution.py:19
  109.1 5.4 %collective-permute-start.16 = (f32[2,8,8,2]{3,2,1,0:T(8,128)S(1)}, f32[2,8,8,2]{3,2,1,0:T(8,128)S(1)}, u32[]{:S(2)}, u32[]{:S(2)}) collective-permute-start(f32[2,8,8,2]{3,2,1,0:T(8,128)S(1)} %get-tuple-element.50), channel_id=1, source_target_pairs={{0,1},{1,2},{2,3},{4,5},{5,6},{6,7},{8,9},{9,10},{10,11},{12,13},{... | collective-permute-start | bytes 3080 | tf_op jit(solution)/shard_map/ppermute | solution.py:17
  112.5 6.2 %collective-permute-start.17 = (f32[2,8,8,2]{3,2,1,0:T(8,128)S(1)}, f32[2,8,8,2]{3,2,1,0:T(8,128)S(1)}, u32[]{:S(2)}, u32[]{:S(2)}) collective-permute-start(f32[2,8,8,2]{3,2,1,0:T(8,128)S(1)} %get-tuple-element.51), channel_id=1, source_target_pairs={{1,0},{2,1},{3,2},{5,4},{6,5},{7,6},{9,8},{10,9},{11,10},{13,12},{... | collective-permute-start | bytes 3080 | tf_op jit(solution)/shard_map/ppermute | solution.py:19
  119.3 2.6 collective-permute-start.18
  120.6 3.1 %collective-permute-start.19 = (f32[2,2,2,16]{3,2,1,0:T(2,128)S(1)}, f32[2,2,2,16]{3,2,1,0:T(2,128)S(1)}, u32[]{:S(2)}, u32[]{:S(2)}) collective-permute-start(f32[2,2,2,16]{3,2,1,0:T(2,128)S(1)} %pad_maximum_fusion.64), channel_id=1, source_target_pairs={{16,0},{17,1},{18,2},{19,3},{20,4},{21,5},{22,6},{23,7},{24,8},{25... | collective-permute-start | bytes 1544 | tf_op jit(solution)/shard_map/ppermute | solution.py:19
  123.7 4.2 %collective-permute-start.20 = (f32[2,6,2,16]{3,2,1,0:T(2,128)S(1)}, f32[2,6,2,16]{3,2,1,0:T(2,128)S(1)}, u32[]{:S(2)}, u32[]{:S(2)}) collective-permute-start(f32[2,6,2,16]{3,2,1,0:T(2,128)S(1)} %pad_maximum_fusion.46), channel_id=1, source_target_pairs={{0,4},{4,8},{8,12},{1,5},{5,9},{9,13},{2,6},{6,10},{10,14},{3,7},{... | collective-permute-start | bytes 4616 | tf_op jit(solution)/shard_map/ppermute | solution.py:17
  126.5 5.6 %collective-permute-start.21 = (f32[2,6,2,16]{3,2,1,0:T(2,128)S(1)}, f32[2,6,2,16]{3,2,1,0:T(2,128)S(1)}, u32[]{:S(2)}, u32[]{:S(2)}) collective-permute-start(f32[2,6,2,16]{3,2,1,0:T(2,128)S(1)} %pad_maximum_fusion.46), channel_id=1, source_target_pairs={{4,0},{8,4},{12,8},{5,1},{9,5},{13,9},{6,2},{10,6},{14,10},{7,3},{... | collective-permute-start | bytes 4616 | tf_op jit(solution)/shard_map/ppermute | solution.py:19
  132.2 3.7 %collective-permute-start.22 = (f32[2,6,6,2]{3,2,1,0:T(8,128)S(1)}, f32[2,6,6,2]{3,2,1,0:T(8,128)S(1)}, u32[]{:S(2)}, u32[]{:S(2)}) collective-permute-start(f32[2,6,6,2]{3,2,1,0:T(8,128)S(1)} %get-tuple-element.59), channel_id=1, source_target_pairs={{0,1},{1,2},{2,3},{4,5},{5,6},{6,7},{8,9},{9,10},{10,11},{12,13},{... | collective-permute-start | bytes 1736 | tf_op jit(solution)/shard_map/ppermute | solution.py:17
  134.2 6.0 %collective-permute-start.23 = (f32[2,6,6,2]{3,2,1,0:T(8,128)S(1)}, f32[2,6,6,2]{3,2,1,0:T(8,128)S(1)}, u32[]{:S(2)}, u32[]{:S(2)}) collective-permute-start(f32[2,6,6,2]{3,2,1,0:T(8,128)S(1)} %get-tuple-element.60), channel_id=1, source_target_pairs={{1,0},{2,1},{3,2},{5,4},{6,5},{7,6},{9,8},{10,9},{11,10},{13,12},{... | collective-permute-start | bytes 1736 | tf_op jit(solution)/shard_map/ppermute | solution.py:19
  178.8 4.3 %collective-permute-start.24 = (f32[1,1,2,16]{3,2,1,0:T(2,128)S(1)}, f32[1,1,2,16]{3,2,1,0:T(2,128)S(1)}, u32[]{:S(2)}, u32[]{:S(2)}) collective-permute-start(f32[1,1,2,16]{3,2,1,0:T(2,128)S(1)} %get-tuple-element.86), channel_id=1, source_target_pairs={{16,0},{17,1},{18,2},{19,3},{20,4},{21,5},{22,6},{23,7},{24,8},{25... | collective-permute-start | bytes 392 | tf_op jit(solution)/shard_map/ppermute | solution.py:19
  180.1 3.8 %collective-permute-start.25 = (f32[1,1,2,16]{3,2,1,0:T(2,128)S(1)}, f32[1,1,2,16]{3,2,1,0:T(2,128)S(1)}, u32[]{:S(2)}, u32[]{:S(2)}) collective-permute-start(f32[1,1,2,16]{3,2,1,0:T(2,128)S(1)} %get-tuple-element.85), channel_id=1, source_target_pairs={{0,16},{1,17},{2,18},{3,19},{4,20},{5,21},{6,22},{7,23},{8,24},{9,... | collective-permute-start | bytes 392 | tf_op jit(solution)/shard_map/ppermute | solution.py:17
  184.0 6.1 %collective-permute-start.26 = (f32[1,4,1,16]{3,2,1,0:T(1,128)S(1)}, f32[1,4,1,16]{3,2,1,0:T(1,128)S(1)}, u32[]{:S(2)}, u32[]{:S(2)}) collective-permute-start(f32[1,4,1,16]{3,2,1,0:T(1,128)S(1)} %get-tuple-element.84), channel_id=1, source_target_pairs={{4,0},{8,4},{12,8},{5,1},{9,5},{13,9},{6,2},{10,6},{14,10},{7,3},{... | collective-permute-start | bytes 776 | tf_op jit(solution)/shard_map/ppermute | solution.py:19
  185.3 6.1 %collective-permute-start.27 = (f32[1,4,1,16]{3,2,1,0:T(1,128)S(1)}, f32[1,4,1,16]{3,2,1,0:T(1,128)S(1)}, u32[]{:S(2)}, u32[]{:S(2)}) collective-permute-start(f32[1,4,1,16]{3,2,1,0:T(1,128)S(1)} %get-tuple-element.83), channel_id=1, source_target_pairs={{0,4},{4,8},{8,12},{1,5},{5,9},{9,13},{2,6},{6,10},{10,14},{3,7},{... | collective-permute-start | bytes 776 | tf_op jit(solution)/shard_map/ppermute | solution.py:17
  191.5 5.9 %collective-permute-start.28 = (f32[1,4,4,1]{3,2,1,0:T(4,128)S(1)}, f32[1,4,4,1]{3,2,1,0:T(4,128)S(1)}, u32[]{:S(2)}, u32[]{:S(2)}) collective-permute-start(f32[1,4,4,1]{3,2,1,0:T(4,128)S(1)} %get-tuple-element.79), channel_id=1, source_target_pairs={{1,0},{2,1},{3,2},{5,4},{6,5},{7,6},{9,8},{10,9},{11,10},{13,12},{... | collective-permute-start | bytes 200 | tf_op jit(solution)/shard_map/ppermute | solution.py:19
  192.8 5.9 %collective-permute-start.29 = (f32[1,4,4,1]{3,2,1,0:T(4,128)S(1)}, f32[1,4,4,1]{3,2,1,0:T(4,128)S(1)}, u32[]{:S(2)}, u32[]{:S(2)}) collective-permute-start(f32[1,4,4,1]{3,2,1,0:T(4,128)S(1)} %get-tuple-element.80), channel_id=1, source_target_pairs={{0,1},{1,2},{2,3},{4,5},{5,6},{6,7},{8,9},{9,10},{10,11},{12,13},{... | collective-permute-start | bytes 200 | tf_op jit(solution)/shard_map/ppermute | solution.py:17
  199.1 4.3 %collective-permute-start.30 = (f32[1,1,4,32]{3,2,1,0:T(4,128)S(1)}, f32[1,1,4,32]{3,2,1,0:T(4,128)S(1)}, u32[]{:S(2)}, u32[]{:S(2)}) collective-permute-start(f32[1,1,4,32]{3,2,1,0:T(4,128)S(1)} %get-tuple-element.78), channel_id=1, source_target_pairs={{16,0},{17,1},{18,2},{19,3},{20,4},{21,5},{22,6},{23,7},{24,8},{25... | collective-permute-start | bytes 1544 | tf_op jit(solution)/shard_map/ppermute | solution.py:19
  200.4 3.8 %collective-permute-start.31 = (f32[1,1,4,32]{3,2,1,0:T(4,128)S(1)}, f32[1,1,4,32]{3,2,1,0:T(4,128)S(1)}, u32[]{:S(2)}, u32[]{:S(2)}) collective-permute-start(f32[1,1,4,32]{3,2,1,0:T(4,128)S(1)} %get-tuple-element.77), channel_id=1, source_target_pairs={{0,16},{1,17},{2,18},{3,19},{4,20},{5,21},{6,22},{7,23},{8,24},{9,... | collective-permute-start | bytes 1544 | tf_op jit(solution)/shard_map/ppermute | solution.py:17
  204.3 6.1 %collective-permute-start.33 = (f32[1,6,1,32]{3,2,1,0:T(1,128)S(1)}, f32[1,6,1,32]{3,2,1,0:T(1,128)S(1)}, u32[]{:S(2)}, u32[]{:S(2)}) collective-permute-start(f32[1,6,1,32]{3,2,1,0:T(1,128)S(1)} %get-tuple-element.75), channel_id=1, source_target_pairs={{0,4},{4,8},{8,12},{1,5},{5,9},{9,13},{2,6},{6,10},{10,14},{3,7},{... | collective-permute-start | bytes 2312 | tf_op jit(solution)/shard_map/ppermute | solution.py:17
  209.1 6.7 %collective-permute-start.32 = (f32[1,6,1,32]{3,2,1,0:T(1,128)S(1)}, f32[1,6,1,32]{3,2,1,0:T(1,128)S(1)}, u32[]{:S(2)}, u32[]{:S(2)}) collective-permute-start(f32[1,6,1,32]{3,2,1,0:T(1,128)S(1)} %get-tuple-element.76), channel_id=1, source_target_pairs={{4,0},{8,4},{12,8},{5,1},{9,5},{13,9},{6,2},{10,6},{14,10},{7,3},{... | collective-permute-start | bytes 2312 | tf_op jit(solution)/shard_map/ppermute | solution.py:19
  215.9 6.1 %collective-permute-start.34 = (f32[1,6,6,1]{3,0,2,1:T(1,128)S(1)}, f32[1,6,6,1]{3,0,2,1:T(1,128)S(1)}, u32[]{:S(2)}, u32[]{:S(2)}) collective-permute-start(f32[1,6,6,1]{3,0,2,1:T(1,128)S(1)} %get-tuple-element.71), channel_id=1, source_target_pairs={{1,0},{2,1},{3,2},{5,4},{6,5},{7,6},{9,8},{10,9},{11,10},{13,12},{... | collective-permute-start | bytes 440 | tf_op jit(solution)/shard_map/ppermute | solution.py:19
  217.2 6.3 %collective-permute-start.35 = (f32[1,6,6,1]{3,0,2,1:T(1,128)S(1)}, f32[1,6,6,1]{3,0,2,1:T(1,128)S(1)}, u32[]{:S(2)}, u32[]{:S(2)}) collective-permute-start(f32[1,6,6,1]{3,0,2,1:T(1,128)S(1)} %get-tuple-element.72), channel_id=1, source_target_pairs={{0,1},{1,2},{2,3},{4,5},{5,6},{6,7},{8,9},{9,10},{10,11},{12,13},{... | collective-permute-start | bytes 440 | tf_op jit(solution)/shard_map/ppermute | solution.py:17
  224.1 4.3 %collective-permute-start.36 = (f32[1,1,8,64]{3,2,1,0:T(8,128)S(1)}, f32[1,1,8,64]{3,2,1,0:T(8,128)S(1)}, u32[]{:S(2)}, u32[]{:S(2)}) collective-permute-start(f32[1,1,8,64]{3,2,1,0:T(8,128)S(1)} %get-tuple-element.64), channel_id=1, source_target_pairs={{16,0},{17,1},{18,2},{19,3},{20,4},{21,5},{22,6},{23,7},{24,8},{25... | collective-permute-start | bytes 6152 | tf_op jit(solution)/shard_map/ppermute | solution.py:19
  225.4 3.8 %collective-permute-start.37 = (f32[1,1,8,64]{3,2,1,0:T(8,128)S(1)}, f32[1,1,8,64]{3,2,1,0:T(8,128)S(1)}, u32[]{:S(2)}, u32[]{:S(2)}) collective-permute-start(f32[1,1,8,64]{3,2,1,0:T(8,128)S(1)} %get-tuple-element.63), channel_id=1, source_target_pairs={{0,16},{1,17},{2,18},{3,19},{4,20},{5,21},{6,22},{7,23},{8,24},{9,... | collective-permute-start | bytes 6152 | tf_op jit(solution)/shard_map/ppermute | solution.py:17
  229.2 6.1 %collective-permute-start.39 = (f32[1,10,1,64]{3,2,1,0:T(1,128)S(1)}, f32[1,10,1,64]{3,2,1,0:T(1,128)S(1)}, u32[]{:S(2)}, u32[]{:S(2)}) collective-permute-start(f32[1,10,1,64]{3,2,1,0:T(1,128)S(1)} %get-tuple-element.61), channel_id=1, source_target_pairs={{0,4},{4,8},{8,12},{1,5},{5,9},{9,13},{2,6},{6,10},{10,14},{3,7},{... | collective-permute-start | bytes 7688 | tf_op jit(solution)/shard_map/ppermute | solution.py:17
  234.1 5.5 %collective-permute-start.38 = (f32[1,10,1,64]{3,2,1,0:T(1,128)S(1)}, f32[1,10,1,64]{3,2,1,0:T(1,128)S(1)}, u32[]{:S(2)}, u32[]{:S(2)}) collective-permute-start(f32[1,10,1,64]{3,2,1,0:T(1,128)S(1)} %get-tuple-element.62), channel_id=1, source_target_pairs={{4,0},{8,4},{12,8},{5,1},{9,5},{13,9},{6,2},{10,6},{14,10},{7,3},{... | collective-permute-start | bytes 7688 | tf_op jit(solution)/shard_map/ppermute | solution.py:19
  239.8 6.3 %collective-permute-start.40 = (f32[1,10,10,1]{3,0,2,1:T(1,128)S(1)}, f32[1,10,10,1]{3,0,2,1:T(1,128)S(1)}, u32[]{:S(2)}, u32[]{:S(2)}) collective-permute-start(f32[1,10,10,1]{3,0,2,1:T(1,128)S(1)} %get-tuple-element.56), channel_id=1, source_target_pairs={{1,0},{2,1},{3,2},{5,4},{6,5},{7,6},{9,8},{10,9},{11,10},{13,12},{... | collective-permute-start | bytes 1208 | tf_op jit(solution)/shard_map/ppermute | solution.py:19
  241.1 6.6 %collective-permute-start.41 = (f32[1,10,10,1]{3,0,2,1:T(1,128)S(1)}, f32[1,10,10,1]{3,0,2,1:T(1,128)S(1)}, u32[]{:S(2)}, u32[]{:S(2)}) collective-permute-start(f32[1,10,10,1]{3,0,2,1:T(1,128)S(1)} %get-tuple-element.57), channel_id=1, source_target_pairs={{0,1},{1,2},{2,3},{4,5},{5,6},{6,7},{8,9},{9,10},{10,11},{12,13},{... | collective-permute-start | bytes 1208 | tf_op jit(solution)/shard_map/ppermute | solution.py:17
  249.1 4.3 %collective-permute-start.42 = (f32[1,1,16,128]{3,2,1,0:T(8,128)S(1)}, f32[1,1,16,128]{3,2,1,0:T(8,128)S(1)}, u32[]{:S(2)}, u32[]{:S(2)}) collective-permute-start(f32[1,1,16,128]{3,2,1,0:T(8,128)S(1)} %get-tuple-element.45), channel_id=1, source_target_pairs={{16,0},{17,1},{18,2},{19,3},{20,4},{21,5},{22,6},{23,7},{24,8},{25... | collective-permute-start | bytes 24584 | tf_op jit(solution)/shard_map/ppermute | solution.py:19
  250.4 3.8 %collective-permute-start.43 = (f32[1,1,16,128]{3,2,1,0:T(8,128)S(1)}, f32[1,1,16,128]{3,2,1,0:T(8,128)S(1)}, u32[]{:S(2)}, u32[]{:S(2)}) collective-permute-start(f32[1,1,16,128]{3,2,1,0:T(8,128)S(1)} %get-tuple-element.44), channel_id=1, source_target_pairs={{0,16},{1,17},{2,18},{3,19},{4,20},{5,21},{6,22},{7,23},{8,24},{9,... | collective-permute-start | bytes 24584 | tf_op jit(solution)/shard_map/ppermute | solution.py:17
  254.2 4.2 %collective-permute-start.45 = (f32[1,18,1,128]{3,2,1,0:T(1,128)S(1)}, f32[1,18,1,128]{3,2,1,0:T(1,128)S(1)}, u32[]{:S(2)}, u32[]{:S(2)}) collective-permute-start(f32[1,18,1,128]{3,2,1,0:T(1,128)S(1)} %get-tuple-element.34), channel_id=1, source_target_pairs={{0,4},{4,8},{8,12},{1,5},{5,9},{9,13},{2,6},{6,10},{10,14},{3,7},{... | collective-permute-start | bytes 27656 | tf_op jit(solution)/shard_map/ppermute | solution.py:17
  257.1 5.6 %collective-permute-start.44 = (f32[1,18,1,128]{3,2,1,0:T(1,128)S(1)}, f32[1,18,1,128]{3,2,1,0:T(1,128)S(1)}, u32[]{:S(2)}, u32[]{:S(2)}) collective-permute-start(f32[1,18,1,128]{3,2,1,0:T(1,128)S(1)} %get-tuple-element.35), channel_id=1, source_target_pairs={{4,0},{8,4},{12,8},{5,1},{9,5},{13,9},{6,2},{10,6},{14,10},{7,3},{... | collective-permute-start | bytes 27656 | tf_op jit(solution)/shard_map/ppermute | solution.py:19
  263.2 7.6 %collective-permute-start.46 = (f32[1,18,18,1]{3,0,2,1:T(1,128)S(1)}, f32[1,18,18,1]{3,0,2,1:T(1,128)S(1)}, u32[]{:S(2)}, u32[]{:S(2)}) collective-permute-start(f32[1,18,18,1]{3,0,2,1:T(1,128)S(1)} %get-tuple-element.32), channel_id=1, source_target_pairs={{1,0},{2,1},{3,2},{5,4},{6,5},{7,6},{9,8},{10,9},{11,10},{13,12},{... | collective-permute-start | bytes 3896 | tf_op jit(solution)/shard_map/ppermute | solution.py:19
  264.5 7.7 %collective-permute-start.47 = (f32[1,18,18,1]{3,0,2,1:T(1,128)S(1)}, f32[1,18,18,1]{3,0,2,1:T(1,128)S(1)}, u32[]{:S(2)}, u32[]{:S(2)}) collective-permute-start(f32[1,18,18,1]{3,0,2,1:T(1,128)S(1)} %get-tuple-element.33), channel_id=1, source_target_pairs={{0,1},{1,2},{2,3},{4,5},{5,6},{6,7},{8,9},{9,10},{10,11},{12,13},{... | collective-permute-start | bytes 3896 | tf_op jit(solution)/shard_map/ppermute | solution.py:17
where the time goes:
time: 276 us; the launch traced here: 274 us
  starting transfers between devices  113 us (41%)
  waiting for transfers between devices  75.2 us (27%)
  blocking collectives  37.6 us (14%)
  local copies, waits for them, and re-layouts  28.9 us (10%)
  other arithmetic  17.9 us (6%)
    ppermute x24, starting transfers between devices, extended(): lax.ppermute(tail, axis, [(i, (i + 1) % count) for i in range(ends)])  81.8 us
    ppermute x24, waiting for transfers between devices, extended(): lax.ppermute(head, axis, [((i + 1) % count, i) for i in range(ends)])  56.4 us
    unnamed x1, blocking collectives  37.6 us
    ppermute x24, starting transfers between devices, extended(): lax.ppermute(head, axis, [((i + 1) % count, i) for i in range(ends)])  31.3 us
    ppermute x24, waiting for transfers between devices, extended(): lax.ppermute(tail, axis, [(i, (i + 1) % count) for i in range(ends)])  18.8 us
    reshape x3, local copies, waits for them, and re-layouts, coarsen(): values.reshape((leading, size_x // 2, 2, size_y // 2, 2, size_z // 2, 2))  11 us
    another operation x1, local copies, waits for them, and re-layouts, coarsen(): values.reshape((leading, size_x // 2, 2, size_y // 2, 2, size_z // 2, 2))  10.5 us
    reduce_sum x8, other arithmetic, coarsen(): return jnp.mean(blocks, axis=(2, 4, 6))  8.76 us
  transfers between devices with their start and end apart: 48, of which 33 were waited for; matrix products, arithmetic and copies ran while one was open for 6% of the time, Pallas kernels for 0%

commit v1 on v0

--- a/solution.py
+++ b/solution.py
@@ -1,6 +1,9 @@
+import functools
 import jax
 import jax.numpy as jnp
 from jax import lax
+from jax.experimental import pallas as pl
+from jax.experimental.pallas import tpu as pltpu
 from jax.sharding import PartitionSpec as P
 
 damping = 0.8
@@ -102,9 +105,542 @@
     return correction
 
 
+K = damping / 6.0
+F32 = jnp.float32
+BF = jnp.bfloat16
+
+
+def iota(shape, dim):
+    return lax.broadcasted_iota(jnp.int32, shape, dim)
+
+
+def pick(condition):
+    return jnp.where(condition, 1.0, 0.0).astype(BF)
+
+
+def sel_dot(values, chosen):
+    high = values.astype(BF)
+    low = (values - high.astype(F32)).astype(BF)
+    return jnp.dot(high, chosen, preferred_element_type=F32) + jnp.dot(
+        low, chosen, preferred_element_type=F32
+    )
+
+
+def around(c):
+    rows, lanes = c.shape
+    return (pltpu.roll(c, 1, 0) + pltpu.roll(c, rows - 1, 0)) + (
+        pltpu.roll(c, 1, 1) + pltpu.roll(c, lanes - 1, 1)
+    )
+
+
+def whole_sum(planes, nz):
+    rows, lanes = planes[0].shape
+    row, lane = iota((rows, lanes), 0), iota((rows, lanes), 1)
+    outs = []
+    for p, c in enumerate(planes):
+        s = jnp.where(row > 0, pltpu.roll(c, 1, 0), 0.0) + jnp.where(
+            row < rows - 1, pltpu.roll(c, rows - 1, 0), 0.0
+        )
+        s = s + (
+            jnp.where(lane > 0, pltpu.roll(c, 1, 1), 0.0)
+            + jnp.where(lane < nz - 1, pltpu.roll(c, lanes - 1, 1), 0.0)
+        )
+        if p > 0:
+            s = s + planes[p - 1]
+        if p < len(planes) - 1:
+            s = s + planes[p + 1]
+        outs.append(s)
+    return outs
+
+
+def kernel(
+    dims, b_ref, w_ref, m_ref, f_ref,
+    V0, W0, U0, V1, W1, U1, TT, T2, A2, T3, T4, P4, P3, E2, P2, P1,
+    SX0, SY0, SZ0, RX0, RY0, RXY0, RZ0,
+    SXv, SYv, SZv, RXv, RYv, RXYv, RZv,
+    SXw, SYw, SZw, RXw, RYw, RXYw, RZw,
+    GM, GW, GB, SW, SB,
+    hs, hr, gs, gr,
+):
+    axes = ("gx", "gy", "gz")
+    ix, iy, iz = (lax.axis_index(a) for a in axes)
+    n = dims[0] * dims[1] * dims[2]
+    me = (ix * dims[1] + iy) * dims[2] + iz
+
+    def place(t):
+        return (t // (dims[1] * dims[2]), (t // dims[2]) % dims[1], t % dims[2])
+
+    def other(k):
+        return lax.rem(me + k, n)
+
+    barrier = pltpu.get_barrier_semaphore()
+    for k in range(1, n):
+        pl.semaphore_signal(
+            barrier, inc=1, device_id=place(other(k)), device_id_type=pl.DeviceIdType.MESH
+        )
+
+    def there(d):
+        ok = None
+        for i, s, c in zip((ix, iy, iz), dims, d):
+            if c:
+                t = (i + c < s) if c > 0 else (i + c >= 0)
+                ok = t if ok is None else jnp.logical_and(ok, t)
+        return ok
+
+    def directions(most):
+        found = []
+        for dx in (-1, 0, 1):
+            for dy in (-1, 0, 1):
+                for dz in (-1, 0, 1):
+                    if 0 < abs(dx) + abs(dy) + abs(dz) <= most:
+                        found.append((dx, dy, dz))
+        return found
+
+    def halo_copy(bufs, which, d):
+        SX, SY, SZ, RX, RY, RXY, RZ, part = bufs
+        dx, dy, dz = d
+        up = lambda c: (c + 1) // 2
+        down = lambda c: (1 - c) // 2
+        if dz:
+            s, r = SZ, RZ.at[1 - dx, 1 - dy, down(dz)]
+        elif dx and dy:
+            rows = SY.shape[2]
+            s = SY.at[up(dy), :, pl.ds(rows - part if dx > 0 else 0, part), :]
+            r = RXY.at[down(dx), down(dy)]
+        elif dx:
+            s, r = SX.at[up(dx)], RX.at[down(dx)]
+        else:
+            s, r = SY.at[up(dy)], RY.at[down(dy)]
+        code = ((1 - dx) * 3 + (1 - dy)) * 3 + (1 - dz)
+        return pltpu.make_async_remote_copy(
+            src_ref=s, dst_ref=r, send_sem=hs.at[which, code], recv_sem=hr.at[which, code],
+            device_id=(ix + dx, iy + dy, iz + dz), device_id_type=pl.DeviceIdType.MESH,
+        )
+
+    def halo_start(bufs, which, most):
+        for d in directions(most):
+            @pl.when(there(d))
+            def _(d=d):
+                halo_copy(bufs, which, d).start()
+
+    def halo_wait(bufs, which, most):
+        for d in directions(most):
+            back = tuple(-c for c in d)
+            @pl.when(there(d))
+            def _(back=back):
+                halo_copy(bufs, which, back).wait_recv()
+
+    def halo_sent(bufs, which, most):
+        for d in directions(most):
+            @pl.when(there(d))
+            def _(d=d):
+                halo_copy(bufs, which, d).wait_send()
+
+    def spread(kind, src, dst, k):
+        return pltpu.make_async_remote_copy(
+            src_ref=src, dst_ref=dst.at[me], send_sem=gs.at[kind, k], recv_sem=gr.at[kind, me],
+            device_id=place(other(k)), device_id_type=pl.DeviceIdType.MESH,
+        )
+
+    def arrive(kind, src, dst):
+        for k in range(1, n):
+            o = other(k)
+            pltpu.make_async_remote_copy(
+                src_ref=src, dst_ref=dst.at[o], send_sem=gs.at[kind, k], recv_sem=gr.at[kind, o],
+                device_id=place(o), device_id_type=pl.DeviceIdType.MESH,
+            ).wait_recv()
+
+    nx, ny = b_ref.shape[0], b_ref.shape[1]
+    hx, hy = nx // 2, ny // 2
+    bufs0 = (SX0, SY0, SZ0, RX0, RY0, RXY0, RZ0, 8)
+    bufsv = (SXv, SYv, SZv, RXv, RYv, RXYv, RZv, 16)
+    bufsw = (SXw, SYw, SZw, RXw, RYw, RXYw, RZw, 16)
+
+    lane16 = iota((ny, 128), 1)
+    packed = jnp.zeros((ny, 128), F32)
+    for x in range(nx):
+        w = w_ref[x]
+        v = K * b_ref[x] / w
+        V0[x + 2, 0:ny, 0:128] = v
+        W0[x + 2, 0:ny, 0:128] = w
+        for a, q in enumerate((v, w)):
+            if x < 2:
+                SX0[0, a, x] = q
+            if x >= nx - 2:
+                SX0[1, a, x - nx + 2] = q
+            SY0[0, a, 2 * x : 2 * x + 2, :] = q[0:2, :]
+            SY0[1, a, 2 * x : 2 * x + 2, :] = q[ny - 2 : ny, :]
+            start = 8 * x + 4 * a
+            moved = pltpu.roll(q, (start + 2) % 128, 1)
+            packed = jnp.where((lane16 >= start) & (lane16 < start + 4), moved, packed)
+    SZ0[...] = packed
+
+    pl.semaphore_wait(barrier, n - 1)
+    halo_start(bufs0, 0, 2)
+
+    halve = pick(iota((128, 128), 0) == 2 * iota((128, 128), 1))
+    halve = halve + pick(iota((128, 128), 0) == 2 * iota((128, 128), 1) + 1)
+
+    def coarsen0(planes):
+        for i in range(hx):
+            TT[i] = planes(2 * i) + planes(2 * i + 1)
+        rows = [
+            TT[i, pl.ds(0, hy, stride=2), :] + TT[i, pl.ds(1, hy, stride=2), :] for i in range(hx)
+        ]
+        return sel_dot(jnp.concatenate(rows, axis=0), halve)
+
+    def coarsen1(planes, SG):
+        for i in range(hx // 2):
+            T2[pl.ds(8 * i, 8), :] = planes(2 * i) + planes(2 * i + 1)
+        for y in range(4):
+            A2[pl.ds(4 * y, 4), :] = (
+                T2[pl.ds(2 * y, 4, stride=8), :] + T2[pl.ds(2 * y + 1, 4, stride=8), :]
+            )
+        TT[0] = sel_dot(A2[...], halve)
+        total = TT[0, 0:4, :]
+        for y in range(1, 4):
+            total = total + pltpu.roll(TT[0, 4 * y : 4 * y + 4, :], 32 * y, 1)
+        return total
+
+    lane8 = iota((8, 128), 1)
+
+    def pack1(bufs, planes):
+        SX, SY, SZ = bufs[:3]
+        out = jnp.zeros((8, 128), F32)
+        for x in range(hx):
+            q = planes[x]
+            if x < 3:
+                SX[0, 0, x] = q
+            if x >= hx - 3:
+                SX[1, 0, x - hx + 3] = q
+            SY[0, 0, 4 * x : 4 * x + 4, :] = q[0:4, :]
+            SY[1, 0, 4 * x : 4 * x + 4, :] = q[4:8, :]
+            s = 16 * x
+            out = jnp.where((lane8 >= s) & (lane8 < s + 3), pltpu.roll(q, (s - 61) % 128, 1), out)
+            out = jnp.where(
+                (lane8 >= s + 3) & (lane8 < s + 6), pltpu.roll(q, (s + 3) % 128, 1), out
+            )
+        SZ[...] = out
+
+    w1 = 0.0625 * coarsen0(lambda x: w_ref[x])
+    w1 = [w1[8 * x : 8 * x + 8, :] for x in range(hx)]
+    pack1(bufsw, w1)
+    halo_start(bufsw, 1, 3)
+    SW[...] = 0.0625 * coarsen1(lambda x: w1[x], SW)
+    GW[me] = SW[...]
+    GM[me] = m_ref[...]
+    for k in range(1, n):
+        spread(0, SW, GW, k).start()
+    for k in range(1, n):
+        spread(1, m_ref, GM, k).start()
+
+    def coords(rows, lanes, cy, cz, by, bz):
+        r, l = iota((rows, lanes), 0), iota((rows, lanes), 1)
+        y = jnp.where(r < cy + (rows - cy) // 2, r, r - rows)
+        z = jnp.where(l < cz + (lanes - cz) // 2, l, l - lanes)
+        gy, gz = y + iy * cy, z + iz * cz
+        ok = (gy >= 0) & (gy < dims[1] * cy) & (gz >= 0) & (gz < dims[2] * cz)
+        near = (y >= -by) & (y < cy + by) & (z >= -bz) & (z < cz + bz)
+        return jnp.where(ok & near, 1, 0)
+
+    def plane_mask(base, x, cx):
+        if 0 <= x < cx:
+            return base > 0
+        gx = x + ix * cx
+        inside = jnp.where((gx >= 0) & (gx < dims[0] * cx), 1, 0)
+        return base * inside > 0
+
+    halo_wait(bufs0, 0, 2)
+    mask0 = coords(24, 256, ny, 128, 2, 2)
+    row8 = iota((8, 128), 0)
+    lane24 = iota((24, 128), 1)
+    for a, D in ((0, V0), (1, W0)):
+        D[0:2, 0:ny, 0:128] = RX0[0, a]
+        D[nx + 2 : nx + 4, 0:ny, 0:128] = RX0[1, a]
+        for x in range(nx):
+            D[x + 2, 16:18, 0:128] = RY0[1, a, 2 * x : 2 * x + 2, :]
+            D[x + 2, 22:24, 0:128] = RY0[0, a, 2 * x : 2 * x + 2, :]
+        D[1, 16:18, 0:128] = RXY0[0, 1, a, 6:8, :]
+        D[1, 22:24, 0:128] = RXY0[0, 0, a, 6:8, :]
+        D[nx + 2, 16:18, 0:128] = RXY0[1, 1, a, 0:2, :]
+        D[nx + 2, 22:24, 0:128] = RXY0[1, 0, a, 0:2, :]
+        for dx in (-1, 0, 1):
+            sides = []
+            for side in (0, 1):
+                mid = RZ0[dx + 1, 1, side]
+                if dx == 0:
+                    edge = jnp.where(row8 < 4, RZ0[1, 2, side, 0:8, :], RZ0[1, 0, side, 8:16, :])
+                else:
+                    edge = jnp.zeros((8, 128), F32)
+                sides.append(jnp.concatenate([mid, edge], axis=0))
+            for x in {-1: (nx - 1,), 0: range(nx), 1: (0,)}[dx]:
+                s = 8 * x + 4 * a
+                D[x + 2 + dx * nx, :, 128:256] = jnp.where(
+                    lane24 < 64,
+                    pltpu.roll(sides[1], (-(s + 2)) % 128, 1),
+                    pltpu.roll(sides[0], (126 - s) % 128, 1),
+                )
+        for p in range(nx + 4):
+            D[p] = jnp.where(plane_mask(mask0, p - 2, nx), D[p], 0.0)
+
+    for p in range(1, nx + 3):
+        c = V0[p]
+        u = 1.2 * c + K * (around(c) + (V0[p - 1] + V0[p + 1]))
+        U0[p] = jnp.where(plane_mask(mask0, p - 2, nx), u, 0.0)
+
+    def own_sum(ref, p):
+        c = ref[p]
+        return around(c)[0:ny, 0:128] + (ref[p - 1, 0:ny, 0:128] + ref[p + 1, 0:ny, 0:128])
+
+    def resid0(x):
+        p = x + 2
+        return b_ref[x] - w_ref[x] * (6.0 * U0[p, 0:ny, 0:128] - own_sum(U0, p))
+
+    b1 = 0.125 * coarsen0(resid0)
+    b1 = [b1[8 * x : 8 * x + 8, :] for x in range(hx)]
+    v1 = [jnp.where(lane8 < 64, K * b1[x] / jnp.where(lane8 < 64, w1[x], 1.0), 0.0) for x in range(hx)]
+    pack1(bufsv, v1)
+    halo_start(bufsv, 2, 3)
+
+    mask1 = coords(16, 128, 8, 64, 3, 3)
+    lane1 = iota((16, 128), 1)
+
+    def assemble1(bufs, planes, D):
+        RX, RY, RXY, RZ = bufs[3:7]
+        for dx in (-1, 0, 1):
+            sides = []
+            for side in (0, 1):
+                edge = jnp.where(row8 < 4, RZ[dx + 1, 2, side], RZ[dx + 1, 0, side])
+                sides.append(jnp.concatenate([RZ[dx + 1, 1, side], edge], axis=0))
+            for x in {-1: range(hx - 3, hx), 0: range(hx), 1: range(3)}[dx]:
+                p = x + 3 + dx * hx
+                if dx == 0:
+                    D[p, 0:8, :] = planes[x]
+                    D[p, 8:12, :] = RY[1, 0, 4 * x : 4 * x + 4, :]
+                    D[p, 12:16, :] = RY[0, 0, 4 * x : 4 * x + 4, :]
+                else:
+                    slot = (dx + 1) // 2
+                    D[p, 0:8, :] = RX[slot, 0, p if dx < 0 else x]
+                    q = 4 * (x - 4 if dx < 0 else x)
+                    D[p, 8:12, :] = RXY[slot, 1, 0, q : q + 4, :]
+                    D[p, 12:16, :] = RXY[slot, 0, 0, q : q + 4, :]
+                s = 16 * x
+                ends = jnp.where(
+                    lane1 < 96,
+                    pltpu.roll(sides[1], (61 - s) % 128, 1),
+                    pltpu.roll(sides[0], (125 - s) % 128, 1),
+                )
+                merged = jnp.where(lane1 < 64, D[p], ends)
+                D[p] = jnp.where(plane_mask(mask1, x + dx * hx, hx), merged, 0.0)
+
+    halo_wait(bufsw, 1, 3)
+    assemble1(bufsw, w1, W1)
+
+    block = lane8 // 32
+    quarter = row8 % 4
+
+    def unpack(G):
+        planes = []
+        for X in range(4 * dims[0]):
+            tiles = []
+            for t in range(dims[1] // 2):
+                rows = []
+                for z in range(dims[2]):
+                    d0 = ((X // 4) * dims[1] + 2 * t) * dims[2] + z
+                    d1 = d0 + dims[2]
+                    q = X % 4
+                    rows.append(
+                        jnp.where(
+                            row8 < 4,
+                            jnp.broadcast_to(G[d0, q : q + 1, :], (8, 128)),
+                            jnp.broadcast_to(G[d1, q : q + 1, :], (8, 128)),
+                        )
+                    )
+                out = None
+                for s in range(4):
+                    pre = rows[s % 4]
+                    for j in range(1, 4):
+                        pre = jnp.where(block == j, rows[(j + s) % 4], pre)
+                    moved = pltpu.roll(pre, 32 * s, 1) if s else pre
+                    out = moved if out is None else jnp.where(block == (quarter + s) % 4, moved, out)
+                tiles.append(out)
+            planes.append(jnp.concatenate(tiles, axis=0))
+        return planes
+
+    def coarsen2(planes):
+        c = len(planes) // 2
+        for i in range(c):
+            T3[i] = planes[2 * i] + planes[2 * i + 1]
+        rows = [T3[i, pl.ds(0, 8, stride=2), :] + T3[i, pl.ds(1, 8, stride=2), :] for i in range(c)]
+        out = sel_dot(jnp.concatenate(rows, axis=0), halve)
+        return [out[8 * i : 8 * i + 8, :] for i in range(c)]
+
+    arrive(0, SW, GW)
+    w2 = unpack(GW)
+    w3 = [0.0625 * q for q in coarsen2(w2)]
+    valid3 = lane8 < 64
+    w3s = [jnp.where(valid3, q, 1.0) for q in w3]
+
+    halo_wait(bufsv, 2, 3)
+    assemble1(bufsv, v1, V1)
+    for p in range(1, hx + 5):
+        c = V1[p]
+        u = 1.2 * c + K * (around(c) + (V1[p - 1] + V1[p + 1]))
+        U1[p] = jnp.where(plane_mask(mask1, p - 3, hx), u, 0.0)
+
+    def resid1(x):
+        p = x + 3
+        s = around(U1[p])[0:8, :] + (U1[p - 1, 0:8, :] + U1[p + 1, 0:8, :])
+        return jnp.where(lane8 < 64, b1[x] - w1[x] * (6.0 * U1[p, 0:8, :] - s), 0.0)
+
+    SB[...] = 0.125 * coarsen1(resid1, SB)
+    GB[me] = SB[...]
+    for k in range(1, n):
+        spread(2, SB, GB, k).start()
+    arrive(1, m_ref, GM)
+    arrive(2, SB, GB)
+
+    b2 = unpack(GB)
+    v2 = [K * b / w for b, w in zip(b2, w2)]
+    u2 = [1.2 * v + K * s for v, s in zip(v2, whole_sum(v2, 128))]
+    r2 = [b - w * (6.0 * u - s) for b, w, u, s in zip(b2, w2, u2, whole_sum(u2, 128))]
+    b3 = [0.125 * q for q in coarsen2(r2)]
+    v3 = [K * b / w for b, w in zip(b3, w3s)]
+    u3 = [jnp.where(valid3, 1.2 * v + K * s, 0.0) for v, s in zip(v3, whole_sum(v3, 64))]
+    r3 = [b - w * (6.0 * u - s) for b, w, u, s in zip(b3, w3, u3, whole_sum(u3, 64))]
+    c4 = len(r3) // 2
+    for i in range(c4):
+        T4[pl.ds(8 * i, 8), :] = r3[2 * i] + r3[2 * i + 1]
+    half = 4 * c4
+    b4 = 0.125 * sel_dot(T4[pl.ds(0, half, stride=2), :] + T4[pl.ds(1, half, stride=2), :], halve)
+    acc = b4
+    for j in range(1, 4):
+        acc = jnp.where(quarter == j, pltpu.roll(b4, 32 * j, 1), acc)
+    low = jnp.sum(jnp.where(row8 < 4, acc, 0.0), axis=0, keepdims=True)
+    high = jnp.sum(jnp.where(row8 >= 4, acc, 0.0), axis=0, keepdims=True)
+    cells = GM.shape[0] * GM.shape[1]
+    matrix = GM[...].reshape((cells, 256))
+    solved = jnp.sum(matrix[:, 0:128] * low + matrix[:, 128:256] * high, axis=1, keepdims=True)
+    hit = (iota((cells, 128), 0) % 32) == iota((cells, 128), 1) // 2
+    e4 = jnp.sum(jnp.where(hit, solved, 0.0).reshape((cells // 32, 32, 128)), axis=1)
+    P4[pl.ds(0, half, stride=2), :] = e4
+    P4[pl.ds(1, half, stride=2), :] = e4
+
+    y3 = [u + w * P4[8 * (i // 2) : 8 * (i // 2) + 8, :] for i, (u, w) in enumerate(zip(u3, w3))]
+    e3 = [
+        jnp.where(valid3, (0.2 * y + v + K * s) / w, 0.0)
+        for y, v, s, w in zip(y3, v3, whole_sum(y3, 64), w3s)
+    ]
+    double = pick(iota((128, 256), 0) == iota((128, 256), 1) // 2)
+    wide3 = sel_dot(jnp.concatenate(e3, axis=0), double[:, 0:128])
+    for i in range(len(e3)):
+        P3[i, pl.ds(0, 8, stride=2), :] = wide3[8 * i : 8 * i + 8, :]
+        P3[i, pl.ds(1, 8, stride=2), :] = wide3[8 * i : 8 * i + 8, :]
+    y2 = [u + w * P3[i // 2] for i, (u, w) in enumerate(zip(u2, w2))]
+    s2 = whole_sum(y2, 128)
+    E2[...] = jnp.zeros_like(E2)
+    for i in range(len(y2)):
+        E2[i + 1, 8:24, :] = (0.2 * y2[i] + v2[i] + K * s2[i]) / w2[i]
+
+    seen = jnp.concatenate([E2[4 * ix + i, pl.ds(6 + 4 * iy, 8), :] for i in range(6)], axis=0)
+    j = iota((128, 128), 1)
+    zl = jnp.where(j < 96, j // 2, j // 2 - 64) + 32 * iz
+    wide2 = sel_dot(seen, pick(iota((128, 128), 0) == zl))
+    for i in range(6):
+        P2[i, pl.ds(0, 8, stride=2), :] = wide2[8 * i : 8 * i + 8, :]
+        P2[i, pl.ds(1, 8, stride=2), :] = wide2[8 * i : 8 * i + 8, :]
+    for p in range(1, hx + 5):
+        U1[p] = U1[p] + W1[p] * pltpu.roll(P2[(p - 3) // 2 + 1], 12, 0)
+    e1 = []
+    for p in range(2, hx + 4):
+        c = U1[p]
+        f = 0.2 * c + V1[p] + K * (around(c) + (U1[p - 1] + U1[p + 1]))
+        inside = plane_mask(mask1, p - 3, hx)
+        e1.append(jnp.where(inside, f, 0.0) / jnp.where(inside, W1[p], 1.0))
+    wide1 = sel_dot(jnp.concatenate(e1, axis=0), double)
+    for i in range(hx + 2):
+        for t in range(2):
+            q = wide1[16 * i : 16 * i + 16, 128 * t : 128 * t + 128]
+            P1[t, i, pl.ds(0, 16, stride=2), :] = q
+            P1[t, i, pl.ds(1, 16, stride=2), :] = q
+
+    for p in range(1, nx + 3):
+        i = (p - 2) // 2 + 1
+        parts = []
+        for t in range(2):
+            edge = jnp.where(row8 < 4, P1[t, i, 16:24, :], P1[t, i, 24:32, :])
+            parts.append(jnp.concatenate([P1[t, i, 0:16, :], edge], axis=0))
+        U0[p] = U0[p] + W0[p] * jnp.concatenate(parts, axis=1)
+    for x in range(nx):
+        p = x + 2
+        f_ref[x] = 0.2 * U0[p, 0:ny, 0:128] + V0[p, 0:ny, 0:128] + K * own_sum(U0, p)
+
+    halo_sent(bufs0, 0, 2)
+    halo_sent(bufsw, 1, 3)
+    halo_sent(bufsv, 2, 3)
+    for k in range(1, n):
+        spread(0, SW, GW, k).wait_send()
+        spread(1, m_ref, GM, k).wait_send()
+        spread(2, SB, GB, k).wait_send()
+
+
+def fused(dims, sources, stiffness, coarse_inverse):
+    nx, ny, nz = stiffness.shape
+    n = dims[0] * dims[1] * dims[2]
+    vm = lambda *s: pltpu.VMEM(s, F32)
+    halo0 = [
+        vm(2, 2, 2, ny, 128), vm(2, 2, 2 * nx, 128), vm(ny, 128),
+        vm(2, 2, 2, ny, 128), vm(2, 2, 2 * nx, 128), vm(2, 2, 2, 8, 128), vm(3, 3, 2, ny, 128),
+    ]
+    halo1 = [
+        vm(2, 1, 3, 8, 128), vm(2, 1, 32, 128), vm(8, 128),
+        vm(2, 1, 3, 8, 128), vm(2, 1, 32, 128), vm(2, 2, 1, 16, 128), vm(3, 3, 2, 8, 128),
+    ]
+    scaled = pl.pallas_call(
+        functools.partial(kernel, dims),
+        out_shape=jax.ShapeDtypeStruct((nx, ny, nz), F32),
+        in_specs=[pl.BlockSpec(memory_space=pltpu.VMEM)] * 3,
+        out_specs=pl.BlockSpec(memory_space=pltpu.VMEM),
+        scratch_shapes=[
+            vm(nx + 4, 24, 256), vm(nx + 4, 24, 256), vm(nx + 4, 24, 256),
+            vm(14, 16, 128), vm(14, 16, 128), vm(14, 16, 128),
+            vm(8, 16, 128), vm(32, 128), vm(16, 128), vm(2 * dims[0], 16, 128),
+            vm(16, 128), vm(16, 128), vm(2 * dims[0], 16, 128),
+            vm(4 * dims[0] + 2, 32, 128), vm(6, 16, 128), vm(2, 10, 32, 128),
+        ]
+        + halo0 + halo1 + halo1
+        + [
+            vm(n, 8, 256), vm(n, 4, 128), vm(n, 4, 128), vm(4, 128), vm(4, 128),
+            pltpu.SemaphoreType.DMA((3, 27)), pltpu.SemaphoreType.DMA((3, 27)),
+            pltpu.SemaphoreType.DMA((3, n)), pltpu.SemaphoreType.DMA((3, n)),
+        ],
+        compiler_params=pltpu.CompilerParams(collective_id=0, has_side_effects=True),
+        name="cycle",
+    )(sources[0], stiffness, coarse_inverse)
+    return (scaled / stiffness)[None]
+
+
 def solution(mesh):
+    dims = tuple(mesh.shape[a] for a in ("gx", "gy", "gz"))
+
+    def run(sources, stiffness, coarse_inverse):
+        nx, ny, nz = stiffness.shape
+        lanes = 128
+        cells = coarse_inverse.shape[1]
+        levels_fit = (
+            sources.shape[0] == 1
+            and nx == ny == 16
+            and nz == lanes
+            and dims[2] * nz == 4 * lanes
+            and dims[1] * ny == 64
+            and cells == 2 * lanes
+        )
+        if levels_fit:
+            return fused(dims, sources, stiffness, coarse_inverse)
+        return per_device(sources, stiffness, coarse_inverse)
+
     in_specs = (P(None, "gx", "gy", "gz"), P("gx", "gy", "gz"), P(("gx", "gy", "gz"), None))
     out_specs = P(None, "gx", "gy", "gz")
     return jax.shard_map(
-        per_device, mesh=mesh, in_specs=in_specs, out_specs=out_specs, check_vma=False
+        run, mesh=mesh, in_specs=in_specs, out_specs=out_specs, check_vma=False
     )

time: 276 us -> 31.2 us (0.11)
  starting transfers between devices: 113 us -> 0 us
  waiting for transfers between devices: 75.2 us -> 0 us
  blocking collectives: 37.6 us -> 0 us
  Pallas kernels: 0 us -> 29.4 us
  local copies, waits for them, and re-layouts: 28.9 us -> 0.01 us
  other arithmetic: 17.9 us -> 1.58 us
    ppermute x48 -> x0, starting transfers between devices: 113 us -> none  [the longest x24 81.8 us: extended(): lax.ppermute(tail, axis, [(i, (i + 1) % count) for i in range(ends)])]
    ppermute x48 -> x0, waiting for transfers between devices: 75.2 us -> none  [the longest x24 56.4 us: extended(): lax.ppermute(head, axis, [((i + 1) % count, i) for i in range(ends)])]
    unnamed x1 -> x0, blocking collectives: 37.6 us -> none
    pallas_call x0 -> x1, Pallas kernels: none -> 29.4 us  [fused(): pl.pallas_call(functools.partial(kernel, dims), out_shape=jax.ShapeDtypeS...]
    reshape x3 -> x0, local copies, waits for them, and re-layouts: 11 us -> none  [coarsen(): values.reshape((leading, size_x // 2, 2, size_y // 2, 2, size_z // 2, 2))]
    another operation x1 -> x0, local copies, waits for them, and re-layouts: 10.5 us -> none  [coarsen(): values.reshape((leading, size_x // 2, 2, size_y // 2, 2, size_z // 2, 2))]
    reduce_sum x8 -> x0, other arithmetic: 8.76 us -> none  [coarsen(): return jnp.mean(blocks, axis=(2, 4, 6))]
    concatenate x23 -> x0, other arithmetic: 4.56 us -> none  [the longest x21 4.55 us: extended(): jnp.concatenate([lax.ppermute(tail, axis, [(i, (i + 1) % count) for i in...]
  transfers between devices with their start and end apart: 48 -> 0, of which waited for: 33 -> 0; matrix products, arithmetic and copies ran while one was open for 6% -> 0% of each run, Pallas kernels for 0% -> 0%
where the time goes in v1:
time: 31.2 us; the launch traced here: 31 us
  Pallas kernels  29.4 us (94%)
  other arithmetic  1.58 us (5%)
    pallas_call x1, Pallas kernels, fused(): pl.pallas_call(functools.partial(kernel, dims), out_shape=jax.ShapeDtypeS...  29.4 us
    broadcast_in_dim x1, other arithmetic, fused(): return (scaled / stiffness)[None]  1.58 us

profile of v1, /device:TPU:0, one launch (start us, length us, event | category | flops | bytes accessed | tf_op | source)
XLA Modules:
  0.0 31.0 jit_solution(9165199845517261860)
XLA Ops:
  0.0 0.0 copy-start
  0.0 29.4 %cycle.1 = f32[16,16,128]{2,1,0:T(8,128)} custom-call(f32[16,16,128]{2,1,0:T(8,128)} %bitcast.3, f32[16,16,128]{2,1,0:T(8,128)} %w_ref.1, f32[8,256]{1,0:T(8,128)} %m_ref.1), custom_call_target="tpu_custom_call" | custom-call | tf_op jit(solution)/shard_map/cycle/pallas_call | solution.py:599
  29.4 0.0 copy-done
  29.4 1.6 %divide_bitcast_fusion = f32[1,16,16,128]{3,2,1,0:T(8,128)} fusion(f32[16,16,128]{2,1,0:T(8,128)} %cycle.1, f32[16,16,128]{2,1,0:T(8,128)S(1)} %copy-done), kind=kLoop, calls=%fused_computation | loop fusion | flops 32768 | bytes 393216 | tf_op jit(solution)/shard_map/broadcast_in_dim | solution.py:620
Async XLA Ops:
  0.0 29.4 %copy-start = (f32[16,16,128]{2,1,0:T(8,128)S(1)}, f32[16,16,128]{2,1,0:T(8,128)}, u32[]{:S(2)}) copy-start(f32[16,16,128]{2,1,0:T(8,128)} %w_ref.1) | copy-start | bytes 393220

commit v2 on v1

--- a/solution.py
+++ b/solution.py
@@ -174,10 +174,6 @@
         return lax.rem(me + k, n)
 
     barrier = pltpu.get_barrier_semaphore()
-    for k in range(1, n):
-        pl.semaphore_signal(
-            barrier, inc=1, device_id=place(other(k)), device_id_type=pl.DeviceIdType.MESH
-        )
 
     def there(d):
         ok = None
@@ -195,6 +191,19 @@
                     if 0 < abs(dx) + abs(dy) + abs(dz) <= most:
                         found.append((dx, dy, dz))
         return found
+
+    for d in directions(3):
+        @pl.when(there(d))
+        def _(d=d):
+            pl.semaphore_signal(
+                barrier, inc=1, device_id=(ix + d[0], iy + d[1], iz + d[2]),
+                device_id_type=pl.DeviceIdType.MESH,
+            )
+
+    def span(i, s):
+        return 1 + jnp.where(i > 0, 1, 0) + jnp.where(i < s - 1, 1, 0)
+
+    greeted = span(ix, dims[0]) * span(iy, dims[1]) * span(iz, dims[2]) - 1
 
     def halo_copy(bufs, which, d):
         SX, SY, SZ, RX, RY, RXY, RZ, part = bufs
@@ -275,7 +284,7 @@
             packed = jnp.where((lane16 >= start) & (lane16 < start + 4), moved, packed)
     SZ0[...] = packed
 
-    pl.semaphore_wait(barrier, n - 1)
+    pl.semaphore_wait(barrier, greeted)
     halo_start(bufs0, 0, 2)
 
     halve = pick(iota((128, 128), 0) == 2 * iota((128, 128), 1))
@@ -325,14 +334,9 @@
     w1 = 0.0625 * coarsen0(lambda x: w_ref[x])
     w1 = [w1[8 * x : 8 * x + 8, :] for x in range(hx)]
     pack1(bufsw, w1)
-    halo_start(bufsw, 1, 3)
     SW[...] = 0.0625 * coarsen1(lambda x: w1[x], SW)
     GW[me] = SW[...]
     GM[me] = m_ref[...]
-    for k in range(1, n):
-        spread(0, SW, GW, k).start()
-    for k in range(1, n):
-        spread(1, m_ref, GM, k).start()
 
     def coords(rows, lanes, cy, cz, by, bz):
         r, l = iota((rows, lanes), 0), iota((rows, lanes), 1)
@@ -351,6 +355,7 @@
         return base * inside > 0
 
     halo_wait(bufs0, 0, 2)
+    halo_start(bufsw, 1, 3)
     mask0 = coords(24, 256, ny, 128, 2, 2)
     row8 = iota((8, 128), 0)
     lane24 = iota((24, 128), 1)
@@ -434,6 +439,10 @@
                 D[p] = jnp.where(plane_mask(mask1, x + dx * hx, hx), merged, 0.0)
 
     halo_wait(bufsw, 1, 3)
+    for k in range(1, n):
+        spread(0, SW, GW, k).start()
+    for k in range(1, n):
+        spread(1, m_ref, GM, k).start()
     assemble1(bufsw, w1, W1)
 
     block = lane8 // 32
@@ -475,11 +484,6 @@
         out = sel_dot(jnp.concatenate(rows, axis=0), halve)
         return [out[8 * i : 8 * i + 8, :] for i in range(c)]
 
-    arrive(0, SW, GW)
-    w2 = unpack(GW)
-    w3 = [0.0625 * q for q in coarsen2(w2)]
-    valid3 = lane8 < 64
-    w3s = [jnp.where(valid3, q, 1.0) for q in w3]
 
     halo_wait(bufsv, 2, 3)
     assemble1(bufsv, v1, V1)
@@ -497,7 +501,11 @@
     GB[me] = SB[...]
     for k in range(1, n):
         spread(2, SB, GB, k).start()
-    arrive(1, m_ref, GM)
+    arrive(0, SW, GW)
+    w2 = unpack(GW)
+    w3 = [0.0625 * q for q in coarsen2(w2)]
+    valid3 = lane8 < 64
+    w3s = [jnp.where(valid3, q, 1.0) for q in w3]
     arrive(2, SB, GB)
 
     b2 = unpack(GB)
@@ -518,6 +526,7 @@
         acc = jnp.where(quarter == j, pltpu.roll(b4, 32 * j, 1), acc)
     low = jnp.sum(jnp.where(row8 < 4, acc, 0.0), axis=0, keepdims=True)
     high = jnp.sum(jnp.where(row8 >= 4, acc, 0.0), axis=0, keepdims=True)
+    arrive(1, m_ref, GM)
     cells = GM.shape[0] * GM.shape[1]
     matrix = GM[...].reshape((cells, 256))
     solved = jnp.sum(matrix[:, 0:128] * low + matrix[:, 128:256] * high, axis=1, keepdims=True)

time: 31.2 us -> 34.6 us (1.11)
  Pallas kernels: 29.4 us -> 32.9 us
    pallas_call x1, Pallas kernels: 29.4 us -> 32.9 us  [fused(): pl.pallas_call(functools.partial(kernel, dims), out_shape=jax.ShapeDtypeS...]
where the time goes in v2:
time: 34.6 us; the launch traced here: 34.5 us
  Pallas kernels  32.9 us (95%)
  other arithmetic  1.58 us (5%)
    pallas_call x1, Pallas kernels, fused(): pl.pallas_call(functools.partial(kernel, dims), out_shape=jax.ShapeDtypeS...  32.9 us
    broadcast_in_dim x1, other arithmetic, fused(): return (scaled / stiffness)[None]  1.58 us

profile of v2, /device:TPU:0, one launch (start us, length us, event | category | flops | bytes accessed | tf_op | source)
XLA Modules:
  0.0 34.5 jit_solution(10010899726533898254)
XLA Ops:
  0.0 0.0 copy-start
  0.0 32.9 %cycle.1 = f32[16,16,128]{2,1,0:T(8,128)} custom-call(f32[16,16,128]{2,1,0:T(8,128)} %bitcast.3, f32[16,16,128]{2,1,0:T(8,128)} %w_ref.1, f32[8,256]{1,0:T(8,128)} %m_ref.1), custom_call_target="tpu_custom_call" | custom-call | tf_op jit(solution)/shard_map/cycle/pallas_call | solution.py:608
  32.9 0.0 copy-done
  32.9 1.6 %divide_bitcast_fusion = f32[1,16,16,128]{3,2,1,0:T(8,128)} fusion(f32[16,16,128]{2,1,0:T(8,128)} %cycle.1, f32[16,16,128]{2,1,0:T(8,128)S(1)} %copy-done), kind=kLoop, calls=%fused_computation | loop fusion | flops 32768 | bytes 393216 | tf_op jit(solution)/shard_map/broadcast_in_dim | solution.py:629
Async XLA Ops:
  0.0 32.9 %copy-start = (f32[16,16,128]{2,1,0:T(8,128)S(1)}, f32[16,16,128]{2,1,0:T(8,128)}, u32[]{:S(2)}) copy-start(f32[16,16,128]{2,1,0:T(8,128)} %w_ref.1) | copy-start | bytes 393220

commit v3 on v2

--- a/solution.py
+++ b/solution.py
@@ -160,7 +160,7 @@
     SXv, SYv, SZv, RXv, RYv, RXYv, RZv,
     SXw, SYw, SZw, RXw, RYw, RXYw, RZw,
     GM, GW, GB, SW, SB,
-    hs, hr, gs, gr,
+    hs, hr, gs, gr, known,
 ):
     axes = ("gx", "gy", "gz")
     ix, iy, iz = (lax.axis_index(a) for a in axes)
@@ -192,13 +192,16 @@
                         found.append((dx, dy, dz))
         return found
 
-    for d in directions(3):
-        @pl.when(there(d))
-        def _(d=d):
-            pl.semaphore_signal(
-                barrier, inc=1, device_id=(ix + d[0], iy + d[1], iz + d[2]),
-                device_id_type=pl.DeviceIdType.MESH,
-            )
+    def greet(sem):
+        for d in directions(3):
+            @pl.when(there(d))
+            def _(d=d):
+                pl.semaphore_signal(
+                    sem, inc=1, device_id=(ix + d[0], iy + d[1], iz + d[2]),
+                    device_id_type=pl.DeviceIdType.MESH,
+                )
+
+    greet(barrier)
 
     def span(i, s):
         return 1 + jnp.where(i > 0, 1, 0) + jnp.where(i < s - 1, 1, 0)
@@ -259,6 +262,24 @@
                 device_id=place(o), device_id_type=pl.DeviceIdType.MESH,
             ).wait_recv()
 
+    group = n // dims[0]
+
+    def beside(k):
+        return ix * group + lax.rem(me - ix * group + k, group)
+
+    def matrix_copy(k, slot):
+        return pltpu.make_async_remote_copy(
+            src_ref=m_ref, dst_ref=GM.at[slot], send_sem=gs.at[1, k], recv_sem=gr.at[1, slot],
+            device_id=place(beside(k)), device_id_type=pl.DeviceIdType.MESH,
+        )
+
+    def matrix_half(x):
+        half = GM.at[pl.ds(x * group, group)]
+        return pltpu.make_async_remote_copy(
+            src_ref=half, dst_ref=half, send_sem=gs.at[3, 0], recv_sem=gr.at[3, 0],
+            device_id=(1 - ix, iy, iz), device_id_type=pl.DeviceIdType.MESH,
+        )
+
     nx, ny = b_ref.shape[0], b_ref.shape[1]
     hx, hy = nx // 2, ny // 2
     bufs0 = (SX0, SY0, SZ0, RX0, RY0, RXY0, RZ0, 8)
@@ -286,6 +307,7 @@
 
     pl.semaphore_wait(barrier, greeted)
     halo_start(bufs0, 0, 2)
+    greet(known.at[0])
 
     halve = pick(iota((128, 128), 0) == 2 * iota((128, 128), 1))
     halve = halve + pick(iota((128, 128), 0) == 2 * iota((128, 128), 1) + 1)
@@ -337,6 +359,9 @@
     SW[...] = 0.0625 * coarsen1(lambda x: w1[x], SW)
     GW[me] = SW[...]
     GM[me] = m_ref[...]
+    halo_start(bufsw, 1, 3)
+    pl.semaphore_wait(known.at[0], greeted)
+    greet(known.at[1])
 
     def coords(rows, lanes, cy, cz, by, bz):
         r, l = iota((rows, lanes), 0), iota((rows, lanes), 1)
@@ -355,7 +380,6 @@
         return base * inside > 0
 
     halo_wait(bufs0, 0, 2)
-    halo_start(bufsw, 1, 3)
     mask0 = coords(24, 256, ny, 128, 2, 2)
     row8 = iota((8, 128), 0)
     lane24 = iota((24, 128), 1)
@@ -406,6 +430,11 @@
     v1 = [jnp.where(lane8 < 64, K * b1[x] / jnp.where(lane8 < 64, w1[x], 1.0), 0.0) for x in range(hx)]
     pack1(bufsv, v1)
     halo_start(bufsv, 2, 3)
+    pl.semaphore_wait(known.at[1], greeted)
+    for k in range(1, n):
+        spread(0, SW, GW, k).start()
+    for k in range(1, group):
+        matrix_copy(k, me).start()
 
     mask1 = coords(16, 128, 8, 64, 3, 3)
     lane1 = iota((16, 128), 1)
@@ -439,10 +468,6 @@
                 D[p] = jnp.where(plane_mask(mask1, x + dx * hx, hx), merged, 0.0)
 
     halo_wait(bufsw, 1, 3)
-    for k in range(1, n):
-        spread(0, SW, GW, k).start()
-    for k in range(1, n):
-        spread(1, m_ref, GM, k).start()
     assemble1(bufsw, w1, W1)
 
     block = lane8 // 32
@@ -506,6 +531,9 @@
     w3 = [0.0625 * q for q in coarsen2(w2)]
     valid3 = lane8 < 64
     w3s = [jnp.where(valid3, q, 1.0) for q in w3]
+    for k in range(1, group):
+        matrix_copy(k, beside(k)).wait_recv()
+    matrix_half(ix).start()
     arrive(2, SB, GB)
 
     b2 = unpack(GB)
@@ -526,7 +554,7 @@
         acc = jnp.where(quarter == j, pltpu.roll(b4, 32 * j, 1), acc)
     low = jnp.sum(jnp.where(row8 < 4, acc, 0.0), axis=0, keepdims=True)
     high = jnp.sum(jnp.where(row8 >= 4, acc, 0.0), axis=0, keepdims=True)
-    arrive(1, m_ref, GM)
+    matrix_half(1 - ix).wait_recv()
     cells = GM.shape[0] * GM.shape[1]
     matrix = GM[...].reshape((cells, 256))
     solved = jnp.sum(matrix[:, 0:128] * low + matrix[:, 128:256] * high, axis=1, keepdims=True)
@@ -589,8 +617,10 @@
     halo_sent(bufsv, 2, 3)
     for k in range(1, n):
         spread(0, SW, GW, k).wait_send()
-        spread(1, m_ref, GM, k).wait_send()
         spread(2, SB, GB, k).wait_send()
+    for k in range(1, group):
+        matrix_copy(k, me).wait_send()
+    matrix_half(ix).wait_send()
 
 
 def fused(dims, sources, stiffness, coarse_inverse):
@@ -621,7 +651,8 @@
         + [
             vm(n, 8, 256), vm(n, 4, 128), vm(n, 4, 128), vm(4, 128), vm(4, 128),
             pltpu.SemaphoreType.DMA((3, 27)), pltpu.SemaphoreType.DMA((3, 27)),
-            pltpu.SemaphoreType.DMA((3, n)), pltpu.SemaphoreType.DMA((3, n)),
+            pltpu.SemaphoreType.DMA((4, n)), pltpu.SemaphoreType.DMA((4, n)),
+            pltpu.SemaphoreType.REGULAR((2,)),
         ],
         compiler_params=pltpu.CompilerParams(collective_id=0, has_side_effects=True),
         name="cycle",
@@ -643,6 +674,7 @@
             and dims[2] * nz == 4 * lanes
             and dims[1] * ny == 64
             and cells == 2 * lanes
+            and dims[0] == 2
         )
         if levels_fit:
             return fused(dims, sources, stiffness, coarse_inverse)

time: 34.6 us -> 30.5 us (0.88)
  Pallas kernels: 32.9 us -> 28.7 us
    pallas_call x1, Pallas kernels: 32.9 us -> 28.7 us  [fused(): pl.pallas_call(functools.partial(kernel, dims), out_shape=jax.ShapeDtypeS...]
where the time goes in v3:
time: 30.5 us; the launch traced here: 30.4 us
  Pallas kernels  28.7 us (94%)
  other arithmetic  1.58 us (5%)
    pallas_call x1, Pallas kernels, fused(): pl.pallas_call(functools.partial(kernel, dims), out_shape=jax.ShapeDtypeS...  28.7 us
    broadcast_in_dim x1, other arithmetic, fused(): return (scaled / stiffness)[None]  1.58 us

profile of v3, /device:TPU:0, one launch (start us, length us, event | category | flops | bytes accessed | tf_op | source)
XLA Modules:
  0.0 30.4 jit_solution(7449456058572031731)
XLA Ops:
  0.0 0.0 copy-start
  0.0 28.7 %cycle.1 = f32[16,16,128]{2,1,0:T(8,128)} custom-call(f32[16,16,128]{2,1,0:T(8,128)} %bitcast.3, f32[16,16,128]{2,1,0:T(8,128)} %w_ref.1, f32[8,256]{1,0:T(8,128)} %m_ref.1), custom_call_target="tpu_custom_call" | custom-call | tf_op jit(solution)/shard_map/cycle/pallas_call | solution.py:638
  28.8 0.0 copy-done
  28.8 1.6 %divide_bitcast_fusion = f32[1,16,16,128]{3,2,1,0:T(8,128)} fusion(f32[16,16,128]{2,1,0:T(8,128)} %cycle.1, f32[16,16,128]{2,1,0:T(8,128)S(1)} %copy-done), kind=kLoop, calls=%fused_computation | loop fusion | flops 32768 | bytes 393216 | tf_op jit(solution)/shard_map/broadcast_in_dim | solution.py:660
Async XLA Ops:
  0.0 28.8 %copy-start = (f32[16,16,128]{2,1,0:T(8,128)S(1)}, f32[16,16,128]{2,1,0:T(8,128)}, u32[]{:S(2)}) copy-start(f32[16,16,128]{2,1,0:T(8,128)} %w_ref.1) | copy-start | bytes 393220
